TPU v7x, 256 devices: a whole 4x4x8 slice. The times are simulated.
256 devices in a mesh: member: 4 (over x), dom: 64 (over y, z, core).
Axes of the slice: x: 4, y: 4, z: 8, core: 2. Of those that a mesh axis runs over, the one named last changes fastest.
Arguments:
- acoustic_perturbation: float32 [4, 32, 65536], P('member', None, 'dom'), may hold values from -8 to 8
- prior_acoustic_state: float32 [4, 32, 65536], P('member', None, 'dom'), may hold values from -8 to 8
- thermal_anomaly: float32 [4, 32, 65536], P('member', None, 'dom'), may hold values from -8 to 8
- model_parameters: float32 [4, 4], P('member'), may hold values from 0.5 to 1.5
- crossing_velocity: float32 [32, 196608], P(None, 'dom'), may hold values from -3 to 3
- face_extent: float32 [196608], P('dom'), may hold values from 0.1 to 0.4
- face_metric_factor: float32 [196608], P('dom'), may hold values from 0.01 to 0.06
- reciprocal_polygon_surface: float32 [65536], P('dom'), may hold values from 0.5 to 2
- owned_totals: int32 [64], P('dom'), may hold values from 768 to 1024, as said below
- export_lists: int32 [64, 6, 128], P('dom'), may hold values from 0 to 1024, as said below
- face_neighbour_pair: int32 [2, 196608], P(None, 'dom'), may hold values from 0 to 1792, as said below
- polygon_side_lookup: int32 [6, 65536], P(None, 'dom'), may hold values from 0 to 3072, as said below
Outputs:
- pressure_out: float32 [4, 32, 65536], P('member', None, 'dom')
- temperature_out: float32 [4, 32, 65536], P('member', None, 'dom')
- ensemble_mean: float32 [32, 65536], P(None, 'dom')
Inputs may be any that keep to these rules, and one draw needn't show every extreme that they name: The first owned_totals[p] cell slots of partition p are its cells, the rest unused; some partition has 1024. Row export_lists[p, b] lists owned cells of partition p sent to partition (p + offsets[b]) mod 64; filled entries first, then 1024 in the empty slots; at least 64 filled entries a row; in every draw some partition receives 128 filled entries in all 6 of its rows. `face_neighbour_pair`: edge 3 i + j of partition p starts at owned cell i and ends at another owned cell or at halo column 1024 + b * 128 + k whose slot k is filled in the sender's row b; edges of unused cells have both ends at 1792. `polygon_side_lookup`: the local edges with an end at each owned cell, 3072 in empty slots; unused cells have only empty slots.
All inputs are finite; a program needn't handle non-finite values.
Results may differ from a plain program's by a relative error of at most 0.0001.
Values sent between devices are 32-bit elements; how exact they have to be, the bound alone decides.
A program may use at most 64 MiB of HBM per device.

v0:
```python
import math

import jax
import jax.numpy as jnp
from jax import lax
from jax.sharding import PartitionSpec as P

STEPS = 2
NS = 3


time_step = 0.25


def passed_along(block, axis, distance):
    devices = range(lax.axis_size(axis))
    route = [((i - distance) % len(devices), i) for i in devices]
    return lax.ppermute(block, axis, route)


def from_everyone(shard, axis):
    copies = jnp.broadcast_to(shard, (lax.axis_size(axis), *shard.shape))
    return lax.all_to_all(copies, axis, split_axis=0, concat_axis=0, tiled=True)


def of_everyone(shard, axis):
    return from_everyone(shard, axis).sum(axis=0)


def together(arrays, axis):
    line, at, gathered = (jnp.concatenate([a.reshape(-1) for a in arrays]), 0, [])
    subtotal = of_everyone(line, axis)
    for a in arrays:
        gathered.append(subtotal[at : at + a.size].reshape(a.shape))
        at += a.size
    return tuple(gathered)


def neighbour_offsets(count):
    return [(block_number // 2 + 1) * (1 - 2 * (block_number % 2)) for block_number in range(count)]


def exact_dot(left_side, right_side):
    return jnp.dot(
        left_side, right_side, precision=lax.Precision.HIGHEST, preferred_element_type=jnp.float32
    )


def edge_block_size(edge_count):
    return math.gcd(edge_count, 384)


def gather_ends(extended, finish):
    edge_count = finish.shape[0]
    block_size = edge_block_size(edge_count)
    column_count = extended.shape[1]
    index_blocks = finish.reshape(edge_count // block_size, block_size)

    def one_block(indices):
        selector = (
            lax.broadcasted_iota(jnp.int32, (column_count, block_size), 0) == indices[None, :]
        ).astype(jnp.float32)
        return exact_dot(extended, selector)

    blocks = lax.map(one_block, index_blocks)
    return jnp.transpose(blocks, (1, 0, 2)).reshape(extended.shape[0], edge_count)


def divergence(fluxes, finish, cell_count):
    levels = fluxes.shape[0]
    edge_count = fluxes.shape[1]
    block_size = edge_block_size(edge_count)
    block_count = edge_count // block_size
    index_blocks = finish.reshape(block_count, block_size)
    flux_blocks = jnp.transpose(fluxes.reshape(levels, block_count, block_size), (1, 0, 2))

    def add_block(total, items):
        indices, flux_piece = items
        selector = (
            indices[:, None] == lax.broadcasted_iota(jnp.int32, (block_size, cell_count), 1)
        ).astype(jnp.float32)
        return (total + exact_dot(flux_piece, selector), None)

    incoming, unused = lax.scan(
        add_block, jnp.zeros((levels, cell_count), jnp.float32), (index_blocks, flux_blocks)
    )
    outgoing = jnp.sum(fluxes.reshape(levels, cell_count, 3), axis=2)
    return outgoing - incoming


def outgoing_rows(fields, export_lists):
    listed = export_lists[0].reshape(-1)
    selector = (
        lax.broadcasted_iota(jnp.int32, (fields.shape[1], listed.shape[0]), 0) == listed[None, :]
    ).astype(jnp.float32)
    chosen = exact_dot(fields, selector)
    zero_column = jnp.zeros((fields.shape[0], 1), jnp.float32)
    return (
        chosen.reshape(fields.shape[0], export_lists.shape[1], export_lists.shape[2]),
        zero_column,
    )


def extend(fields, export_lists):
    outgoing, zero_column = outgoing_rows(fields, export_lists)
    dom_count = lax.axis_size("dom")
    pieces = []
    for block_number, offset in enumerate(neighbour_offsets(export_lists.shape[1])):
        pieces.append(passed_along(outgoing[:, block_number], "dom", offset % dom_count))
    return jnp.concatenate([fields] + pieces + [zero_column], axis=1)


def starts_of(fields):
    levels = fields.shape[0]
    cell_count = fields.shape[1]
    return jnp.broadcast_to(fields[:, :, None], (levels, cell_count, 3)).reshape(
        levels, 3 * cell_count
    )


def per_device(
    acoustic_perturbation,
    prior_acoustic_state,
    thermal_anomaly,
    model_parameters,
    crossing_velocity,
    face_extent,
    face_metric_factor,
    reciprocal_polygon_surface,
    owned_totals,
    export_lists,
    face_neighbour_pair,
    polygon_side_lookup,
):
    levels = acoustic_perturbation.shape[1]
    cell_count = acoustic_perturbation.shape[2]
    current = acoustic_perturbation[0]
    previous = prior_acoustic_state[0]
    scalar_quantity = thermal_anomaly[0]
    speed = model_parameters[0, 0]
    kappa = 0.5 * model_parameters[0, 1]
    mixing = 0.6 * model_parameters[0, 2]
    couple = model_parameters[0, 3]
    owned = (jnp.arange(cell_count, dtype=jnp.int32) < owned_totals[0])[None, :]
    cell_area = jnp.where(owned[0], 1.0 / reciprocal_polygon_surface, 0.0)
    finish = face_neighbour_pair[1]
    inverse = reciprocal_polygon_surface[None, :]
    for outer_step in range(STEPS):
        extended = extend(jnp.concatenate([scalar_quantity, current], axis=0), export_lists)
        theta_ext = extended[:levels]
        press_ext = extended[levels:]
        left = starts_of(scalar_quantity)
        right = gather_ends(theta_ext, finish)
        fluxes = face_extent[None, :] * (
            0.5 * crossing_velocity * (left + right)
            - (0.5 * jnp.abs(crossing_velocity) + kappa) * (right - left)
        )
        differences = scalar_quantity[1:] - scalar_quantity[:-1]
        zero_row = jnp.zeros((1, cell_count), jnp.float32)
        vertical = mixing * (
            jnp.concatenate([differences, zero_row], 0)
            - jnp.concatenate([zero_row, differences], 0)
        )
        advanced = jnp.where(
            owned,
            scalar_quantity
            + time_step * (-inverse * divergence(fluxes, finish, cell_count) + vertical),
            scalar_quantity,
        )
        forcing = couple * (advanced - scalar_quantity) / NS
        for substep in range(NS):
            if substep > 0:
                press_ext = extend(current, export_lists)
            gradient = face_metric_factor[None, :] * (
                gather_ends(press_ext, finish) - starts_of(current)
            )
            stepped = jnp.where(
                owned,
                2.0 * current
                - previous
                + speed * inverse * divergence(gradient, finish, cell_count)
                + forcing,
                current,
            )
            previous, current = (current, stepped)
        weighted, area_total = together(
            (jnp.sum(current * cell_area[None, :], axis=1), jnp.sum(cell_area)), "dom"
        )
        level_mean = (weighted / area_total)[:, None]
        current = jnp.where(owned, current - level_mean, current)
        previous = jnp.where(owned, previous - level_mean, previous)
        scalar_quantity = advanced
    ensemble = of_everyone(current, "member") / lax.axis_size("member")
    return (current[None], scalar_quantity[None], ensemble)


def solution(mesh):
    in_specs = (
        P("member", None, "dom"),
        P("member", None, "dom"),
        P("member", None, "dom"),
        P("member", None),
        P(None, "dom"),
        P("dom"),
        P("dom"),
        P("dom"),
        P("dom"),
        P("dom", None, None),
        P(None, "dom"),
        P(None, "dom"),
    )
    out_specs = (P("member", None, "dom"), P("member", None, "dom"), P(None, "dom"))
    return jax.shard_map(
        per_device, mesh=mesh, in_specs=in_specs, out_specs=out_specs, check_vma=False
    )
```

profile of v0, /device:TPU:1, one launch (start us, length us, event | category | flops | bytes accessed | tf_op | source)
XLA Modules:
  0.0 603.9 jit_solution(9445253510861319733)
XLA Ops:
  11.7 4.9 collective-permute-start.3
  25.2 3.8 reshape.222
  37.0 5.3 collective-permute-start.5
  55.0 9.1 %while.168 = (s32[]{:T(128)}, f32[8,32,384]{2,1,0:T(8,128)S(1)}, s32[8,384]{1,0:T(8,128)S(1)}, f32[32,1793]{1,0:T(8,128)S(1)}, s32[]{:T(128)}) while((s32[]{:T(128)}, f32[8,32,384]{2,1,0:T(8,128)S(1)}, s32[8,384]{1,0:T(8,128)S(1)}, f32[32,1793]{1,0:T(8,128)S(1)}, s32[]{:T(128)}) %tuple.384), condition=%wide.region_1.2_spmd, body=%wide.region_0.1_spmd.sunk | while | flops 265077120 | bytes 300101 | solution.py:65
  64.6 3.0 multiply_bitcast_fusion.5
  69.5 23.0 %while.176 = (s32[]{:T(128)}, f32[32,1024]{1,0:T(8,128)}, f32[8,32,384]{2,1,0:T(8,128)S(1)}, s32[8,384]{1,0:T(8,128)S(1)}, s32[]{:T(128)}, /*index=5*/s32[]{:T(128)}) while((s32[]{:T(128)}, f32[32,1024]{1,0:T(8,128)}, f32[8,32,384]{2,1,0:T(8,128)S(1)}, s32[8,384]{1,0:T(8,128)S(1)}, s32[]{:T(128)}, /*index=5*/s32[]{:T(128)}) %tuple.432), condition=%wide.region_4.5_spmd.clone, body=%wide.region_3.4_spmd.clone.sunk | while | flops 151453696 | bytes 315991 | solution.py:84
  96.6 16.6 %while.169 = (s32[]{:T(128)}, f32[8,32,384]{2,1,0:T(8,128)S(1)}, s32[8,384]{1,0:T(8,128)S(1)}, f32[32,1793]{1,0:T(8,128)}, s32[]{:T(128)}) while((s32[]{:T(128)}, f32[8,32,384]{2,1,0:T(8,128)S(1)}, s32[8,384]{1,0:T(8,128)S(1)}, f32[32,1793]{1,0:T(8,128)}, s32[]{:T(128)}) %tuple.433), condition=%wide.region_6.7_spmd, body=%wide.region_5.6_spmd.sunk | while | flops 265077120 | bytes 283845 | solution.py:65
  117.0 25.9 %while.177 = (s32[]{:T(128)}, f32[32,1024]{1,0:T(8,128)}, f32[8,32,384]{2,0,1:T(8,128)}, s32[8,384]{1,0:T(8,128)S(1)}, s32[]{:T(128)}, /*index=5*/s32[]{:T(128)}) while((s32[]{:T(128)}, f32[32,1024]{1,0:T(8,128)}, f32[8,32,384]{2,0,1:T(8,128)}, s32[8,384]{1,0:T(8,128)S(1)}, s32[]{:T(128)}, /*index=5*/s32[]{:T(128)}) %tuple.447), condition=%wide.region_9.10_spmd.clone, body=%wide.region_8.9_spmd.clone.sunk | while | flops 151453696 | bytes 414295 | solution.py:84
  146.5 3.7 reshape.225
  150.2 7.6 %multiply_reduce_fusion.5 = f32[32,1024]{0,1:T(8,128)} fusion(f32[32,1024,3]{0,2,1:T(4,128)} %reshape.221, f32[32,1024]{0,1:T(8,128)S(1)} %bitcast.287, f32[1024,3]{1,0:T(8,128)S(1)} %mul.239), kind=kLoop, calls=%fused_computation.122 | loop fusion | flops 262144 | bytes 667648 | tf_op jit(solution)/shard_map/reduce_sum | solution.py:87
  157.8 3.7 reduce_sum.131
  161.5 3.4 fusion.93
  169.6 3.7 collective-permute-start.7
  173.3 4.8 collective-permute-start.9
  179.8 3.8 reshape.229
  183.6 5.2 collective-permute-start.11
  193.2 16.6 %while.170 = (s32[]{:T(128)}, f32[8,32,384]{2,1,0:T(8,128)S(1)}, s32[8,384]{1,0:T(8,128)S(1)}, f32[32,1793]{1,0:T(8,128)}, s32[]{:T(128)}) while((s32[]{:T(128)}, f32[8,32,384]{2,1,0:T(8,128)S(1)}, s32[8,384]{1,0:T(8,128)S(1)}, f32[32,1793]{1,0:T(8,128)}, s32[]{:T(128)}) %tuple.435), condition=%wide.region_11.12_spmd, body=%wide.region_10.11_spmd.sunk | while | flops 265077120 | bytes 283845 | solution.py:65
  211.4 3.5 multiply_bitcast_fusion.4
  216.8 6.2 %while.178 = (s32[]{:T(128)}, f32[32,1024]{1,0:T(8,128)S(1)}, f32[8,32,384]{2,1,0:T(8,128)S(1)}, s32[8,384]{1,0:T(8,128)S(1)}, s32[]{:T(128)}, /*index=5*/s32[]{:T(128)}) while((s32[]{:T(128)}, f32[32,1024]{1,0:T(8,128)S(1)}, f32[8,32,384]{2,1,0:T(8,128)S(1)}, s32[8,384]{1,0:T(8,128)S(1)}, s32[]{:T(128)}, ...), condition=%wide.region_14.15_spmd.clone, body=%wide.region_13.14_spmd.clone.sunk | while | flops 151453696 | bytes 316503 | solution.py:84
  224.0 3.7 reshape.228
  227.7 6.9 %multiply_reduce_fusion.4 = f32[32,1024]{0,1:T(8,128)S(1)} fusion(f32[32,1024,3]{0,2,1:T(4,128)} %reshape.228, f32[32,1024]{0,1:T(8,128)S(1)} %get-tuple-element.982, f32[1024,3]{1,0:T(8,128)S(1)} %mul.239), kind=kLoop, calls=%fused_computation.121 | loop fusion | flops 262144 | bytes 667648 | tf_op jit(solution)/shard_map/reduce_sum | solution.py:87
  239.3 3.8 collective-permute-start.13
  243.1 4.8 collective-permute-start.15
  249.7 3.8 reshape.232
  253.5 5.2 collective-permute-start.17
  259.6 9.0 %while.171 = (s32[]{:T(128)}, f32[8,32,384]{2,1,0:T(8,128)S(1)}, s32[8,384]{1,0:T(8,128)S(1)}, f32[32,1793]{1,0:T(8,128)S(1)}, s32[]{:T(128)}) while((s32[]{:T(128)}, f32[8,32,384]{2,1,0:T(8,128)S(1)}, s32[8,384]{1,0:T(8,128)S(1)}, f32[32,1793]{1,0:T(8,128)S(1)}, s32[]{:T(128)}) %tuple.437), condition=%wide.region_16.17_spmd, body=%wide.region_15.16_spmd.sunk | while | flops 265077120 | bytes 300101 | solution.py:65
  270.3 3.5 multiply_bitcast_fusion.3
  275.7 6.2 %while.179 = (s32[]{:T(128)}, f32[32,1024]{1,0:T(8,128)S(1)}, f32[8,32,384]{2,1,0:T(8,128)S(1)}, s32[8,384]{1,0:T(8,128)S(1)}, s32[]{:T(128)}, /*index=5*/s32[]{:T(128)}) while((s32[]{:T(128)}, f32[32,1024]{1,0:T(8,128)S(1)}, f32[8,32,384]{2,1,0:T(8,128)S(1)}, s32[8,384]{1,0:T(8,128)S(1)}, s32[]{:T(128)}, ...), condition=%wide.region_19.20_spmd.clone, body=%wide.region_18.19_spmd.clone.sunk | while | flops 151453696 | bytes 316503 | solution.py:84
  282.9 3.7 reshape.231
  286.6 6.9 %multiply_reduce_fusion.3 = f32[32,1024]{0,1:T(8,128)S(1)} fusion(f32[32,1024,3]{0,2,1:T(4,128)} %reshape.231, f32[32,1024]{0,1:T(8,128)S(1)} %add_select_fusion.5, f32[1024,3]{1,0:T(8,128)S(1)} %mul.239), kind=kLoop, calls=%fused_computation.120 | loop fusion | flops 262144 | bytes 667648 | tf_op jit(solution)/shard_map/reduce_sum | solution.py:87
  295.8 15.0 %all-to-all-start = ((f32[64,1,33]{2,1,0:T(1,128)}), f32[64,1,33]{2,1,0:T(1,128)S(1)}, u32[]{:S(2)}, u32[]{:S(2)}) async-start(f32[64,1,33]{2,1,0:T(1,128)} %broadcast_in_dim.164), calls=%async_computation | async-start | bytes 65536 | tf_op jit(solution)/shard_map/all_to_all | solution.py:23
  313.5 3.8 reshape.238
  328.7 3.6 collective-permute-start.21
  334.0 3.8 reshape.237
  337.8 5.1 collective-permute-start.23
  347.9 3.0 fusion.99
  353.2 17.0 %while.173 = (s32[]{:T(128)}, f32[8,32,384]{2,1,0:T(8,128)S(1)}, s32[8,384]{1,0:T(8,128)S(1)}, f32[32,1793]{1,0:T(8,128)}, s32[]{:T(128)}) while((s32[]{:T(128)}, f32[8,32,384]{2,1,0:T(8,128)S(1)}, s32[8,384]{1,0:T(8,128)S(1)}, f32[32,1793]{1,0:T(8,128)}, s32[]{:T(128)}) %tuple.439), condition=%wide.region_29.30_spmd, body=%wide.region_28.29_spmd.sunk | while | flops 265077120 | bytes 283845 | solution.py:65
  373.1 3.7 reshape.240
  377.6 14.6 %while.181 = (s32[]{:T(128)}, f32[32,1024]{1,0:T(8,128)S(1)}, f32[8,32,384]{2,0,1:T(8,128)}, s32[8,384]{1,0:T(8,128)S(1)}, s32[]{:T(128)}, /*index=5*/s32[]{:T(128)}) while((s32[]{:T(128)}, f32[32,1024]{1,0:T(8,128)S(1)}, f32[8,32,384]{2,0,1:T(8,128)}, s32[8,384]{1,0:T(8,128)S(1)}, s32[]{:T(128)}, /*index=5*/s32[]{:T(128)}) %tuple.451), condition=%wide.region_32.33_spmd.clone, body=%wide.region_31.32_spmd.clone.sunk | while | flops 151453696 | bytes 414295 | solution.py:84
  394.7 9.1 %while.172 = (s32[]{:T(128)}, f32[8,32,384]{2,1,0:T(8,128)S(1)}, s32[8,384]{1,0:T(8,128)S(1)}, f32[32,1793]{1,0:T(8,128)S(1)}, s32[]{:T(128)}) while((s32[]{:T(128)}, f32[8,32,384]{2,1,0:T(8,128)S(1)}, s32[8,384]{1,0:T(8,128)S(1)}, f32[32,1793]{1,0:T(8,128)S(1)}, s32[]{:T(128)}) %tuple.441), condition=%wide.region_24.25_spmd, body=%wide.region_23.24_spmd.sunk | while | flops 265077120 | bytes 300101 | solution.py:65
  405.5 3.5 multiply_bitcast_fusion.2
  410.8 6.2 %while.180 = (s32[]{:T(128)}, f32[32,1024]{1,0:T(8,128)S(1)}, f32[8,32,384]{2,1,0:T(8,128)S(1)}, s32[8,384]{1,0:T(8,128)S(1)}, s32[]{:T(128)}, /*index=5*/s32[]{:T(128)}) while((s32[]{:T(128)}, f32[32,1024]{1,0:T(8,128)S(1)}, f32[8,32,384]{2,1,0:T(8,128)S(1)}, s32[8,384]{1,0:T(8,128)S(1)}, s32[]{:T(128)}, ...), condition=%wide.region_27.28_spmd.clone, body=%wide.region_26.27_spmd.clone.sunk | while | flops 151453696 | bytes 316503 | solution.py:84
  418.1 3.6 reshape.236
  421.8 7.6 %multiply_reduce_fusion.2 = f32[32,1024]{0,1:T(8,128)} fusion(f32[32,1024,3]{0,2,1:T(4,128)} %reshape.236, f32[32,1024]{0,1:T(8,128)S(1)} %subtract_select_fusion.2, f32[1024,3]{1,0:T(8,128)S(1)} %mul.239), kind=kLoop, calls=%fused_computation.119 | loop fusion | flops 262144 | bytes 667648 | tf_op jit(solution)/shard_map/reduce_sum | solution.py:87
  429.4 3.7 reduce_sum.138
  433.2 3.5 fusion.89
  440.8 3.7 collective-permute-start.25
  444.6 4.8 collective-permute-start.27
  451.4 5.2 collective-permute-start.29
  458.9 9.1 %while.174 = (s32[]{:T(128)}, f32[8,32,384]{2,1,0:T(8,128)S(1)}, s32[8,384]{1,0:T(8,128)S(1)}, f32[32,1793]{1,0:T(8,128)S(1)}, s32[]{:T(128)}) while((s32[]{:T(128)}, f32[8,32,384]{2,1,0:T(8,128)S(1)}, s32[8,384]{1,0:T(8,128)S(1)}, f32[32,1793]{1,0:T(8,128)S(1)}, s32[]{:T(128)}) %tuple.443), condition=%wide.region_34.35_spmd, body=%wide.region_33.34_spmd.sunk | while | flops 265077120 | bytes 300101 | solution.py:65
  468.4 3.1 multiply_bitcast_fusion.1
  473.4 6.2 %while.182 = (s32[]{:T(128)}, f32[32,1024]{1,0:T(8,128)S(1)}, f32[8,32,384]{2,1,0:T(8,128)S(1)}, s32[8,384]{1,0:T(8,128)S(1)}, s32[]{:T(128)}, /*index=5*/s32[]{:T(128)}) while((s32[]{:T(128)}, f32[32,1024]{1,0:T(8,128)S(1)}, f32[8,32,384]{2,1,0:T(8,128)S(1)}, s32[8,384]{1,0:T(8,128)S(1)}, s32[]{:T(128)}, ...), condition=%wide.region_37.38_spmd.clone, body=%wide.region_36.37_spmd.clone.sunk | while | flops 151453696 | bytes 316503 | solution.py:84
  482.3 7.0 %multiply_reduce_fusion.1 = f32[32,1024]{0,1:T(8,128)S(1)} fusion(f32[32,1024,3]{0,2,1:T(4,128)} %reshape.243, f32[32,1024]{0,1:T(8,128)S(1)} %get-tuple-element.975, f32[1024,3]{1,0:T(8,128)S(1)} %mul.239), kind=kLoop, calls=%fused_computation.118 | loop fusion | flops 262144 | bytes 667648 | tf_op jit(solution)/shard_map/reduce_sum | solution.py:87
  494.0 3.8 collective-permute-start.31
  497.8 4.8 collective-permute-start.33
  504.3 3.8 reshape.247
  508.2 5.2 collective-permute-start.35
  514.2 9.0 %while.175 = (s32[]{:T(128)}, f32[8,32,384]{2,1,0:T(8,128)S(1)}, s32[8,384]{1,0:T(8,128)S(1)}, f32[32,1793]{1,0:T(8,128)S(1)}, s32[]{:T(128)}) while((s32[]{:T(128)}, f32[8,32,384]{2,1,0:T(8,128)S(1)}, s32[8,384]{1,0:T(8,128)S(1)}, f32[32,1793]{1,0:T(8,128)S(1)}, s32[]{:T(128)}) %tuple.445), condition=%wide.region_39.40_spmd, body=%wide.region_38.39_spmd.sunk | while | flops 265077120 | bytes 300101 | solution.py:65
  523.8 3.0 multiply_bitcast_fusion
  528.6 22.9 %while.183 = (s32[]{:T(128)}, f32[32,1024]{1,0:T(8,128)}, f32[8,32,384]{2,1,0:T(8,128)S(1)}, s32[8,384]{1,0:T(8,128)S(1)}, s32[]{:T(128)}, /*index=5*/s32[]{:T(128)}) while((s32[]{:T(128)}, f32[32,1024]{1,0:T(8,128)}, f32[8,32,384]{2,1,0:T(8,128)S(1)}, s32[8,384]{1,0:T(8,128)S(1)}, s32[]{:T(128)}, /*index=5*/s32[]{:T(128)}) %tuple.446), condition=%wide.region_42.43_spmd.clone, body=%wide.region_41.42_spmd.clone.sunk | while | flops 151453696 | bytes 315991 | solution.py:84
  555.2 6.9 %multiply_reduce_fusion = f32[32,1024]{0,1:T(8,128)S(1)} fusion(f32[32,1024,3]{0,2,1:T(4,128)} %reshape.246, f32[32,1024]{0,1:T(8,128)S(1)} %add_select_fusion.3, f32[1024,3]{1,0:T(8,128)S(1)} %mul.239), kind=kLoop, calls=%fused_computation.117 | loop fusion | flops 262144 | bytes 667648 | tf_op jit(solution)/shard_map/reduce_sum | solution.py:87
  563.8 23.8 %all_to_all.17 = f32[64,1,33]{2,1,0:T(1,128)S(1)} all-to-all(f32[64,1,33]{2,1,0:T(1,128)S(1)} %broadcast_in_dim.169), channel_id=1, replica_groups=mesh['member'=4,'dom'=64] {'dom'}, dimensions={0} | all-to-all | bytes 16896 | tf_op jit(solution)/shard_map/all_to_all | solution.py:23
  590.2 4.0 all-to-all-start.2
  596.1 6.5 %all-to-all-done.2 = f32[4,32,1024]{2,1,0:T(8,128)S(1)} async-done(((f32[4,32,1024]{2,1,0:T(8,128)}), f32[4,32,1024]{2,1,0:T(8,128)S(1)}, u32[]{:S(2)}, u32[]{:S(2)}) %all-to-all-start.2) | async-done | bytes 524320 | tf_op jit(solution)/shard_map/all_to_all | solution.py:23
  (590 shorter events, 352.2 us)
Async XLA Ops:
  3.6 14.1 %copy-start.36 = (s32[6,128]{1,0:T(8,128)}, s32[6,128]{1,0:T(8,128)S(1)}, u32[]{:S(2)}) copy-start(s32[6,128]{1,0:T(8,128)S(1)} %reduce.19) | copy-start | bytes 9220
  6.4 12.3 %copy-start.32 = (s32[2,3072]{1,0:T(2,128)S(1)}, s32[2,3072]{1,0:T(2,128)}, u32[]{:S(2)}) copy-start(s32[2,3072]{1,0:T(2,128)} %param.54) | copy-start | bytes 73732
  6.4 12.3 %copy-start.31 = (f32[1,4]{1,0:T(1,128)S(1)}, f32[1,4]{1,0:T(1,128)}, u32[]{:S(2)}) copy-start(f32[1,4]{1,0:T(1,128)} %param.47) | copy-start | bytes 52
  6.4 13.6 %copy-start.42 = (f32[1024]{0:T(1024)S(1)}, f32[1024]{0:T(1024)}, u32[]{:S(2)}) copy-start(f32[1024]{0:T(1024)} %param.51) | copy-start | bytes 12292
  6.4 16.0 %copy-start.26 = (f32[3072]{0:T(1024)S(1)}, f32[3072]{0:T(1024)}, u32[]{:S(2)}) copy-start(f32[3072]{0:T(1024)} %param.50) | copy-start | bytes 36868
  7.1 29.9 %collective-permute-start = (f32[64,128]{0,1:T(8,128)}, f32[64,128]{0,1:T(8,128)}, u32[]{:S(2)}, u32[]{:S(2)}) collective-permute-start(f32[64,128]{0,1:T(8,128)} %get-tuple-element.1000), channel_id=1, source_target_pairs={{63,0},{0,1},{1,2},{2,3},{3,4},{4,5},{5,6},{6,7},{7,8},{8,9},{9,10... | collective-permute-start | bytes 98312 | tf_op jit(solution)/shard_map/ppermute | solution.py:18
  10.1 33.6 %collective-permute-start.1 = (f32[64,128]{0,1:T(8,128)}, f32[64,128]{0,1:T(8,128)}, u32[]{:S(2)}, u32[]{:S(2)}) collective-permute-start(f32[64,128]{0,1:T(8,128)} %get-tuple-element.999), channel_id=1, source_target_pairs={{1,0},{2,1},{3,2},{4,3},{5,4},{6,5},{7,6},{8,7},{9,8},{10,9},{11,1... | collective-permute-start | bytes 98312 | tf_op jit(solution)/shard_map/ppermute | solution.py:18
  10.3 34.9 %collective-permute-start.2 = (f32[64,128]{0,1:T(8,128)S(1)}, f32[64,128]{0,1:T(8,128)}, u32[]{:S(2)}, u32[]{:S(2)}) collective-permute-start(f32[64,128]{0,1:T(8,128)S(1)} %get-tuple-element.998), channel_id=1, source_target_pairs={{62,0},{63,1},{0,2},{1,3},{2,4},{3,5},{4,6},{5,7},{6,8},{7,9},{8,1... | collective-permute-start | bytes 98312 | tf_op jit(solution)/shard_map/ppermute | solution.py:18
  11.7 34.9 %collective-permute-start.3 = (f32[64,128]{0,1:T(8,128)S(1)}, f32[64,128]{0,1:T(8,128)}, u32[]{:S(2)}, u32[]{:S(2)}) collective-permute-start(f32[64,128]{0,1:T(8,128)S(1)} %get-tuple-element.997), channel_id=1, source_target_pairs={{2,0},{3,1},{4,2},{5,3},{6,4},{7,5},{8,6},{9,7},{10,8},{11,9},{12,... | collective-permute-start | bytes 98312 | tf_op jit(solution)/shard_map/ppermute | solution.py:18
  16.6 31.5 %collective-permute-start.4 = (f32[64,128]{0,1:T(8,128)S(1)}, f32[64,128]{0,1:T(8,128)}, u32[]{:S(2)}, u32[]{:S(2)}) collective-permute-start(f32[64,128]{0,1:T(8,128)S(1)} %get-tuple-element.996), channel_id=1, source_target_pairs={{61,0},{62,1},{63,2},{0,3},{1,4},{2,5},{3,6},{4,7},{5,8},{6,9},{7,... | collective-permute-start | bytes 98312 | tf_op jit(solution)/shard_map/ppermute | solution.py:18
  37.0 12.6 %collective-permute-start.5 = (f32[64,128]{0,1:T(8,128)S(1)}, f32[64,128]{0,1:T(8,128)S(1)}, u32[]{:S(2)}, u32[]{:S(2)}) collective-permute-start(f32[64,128]{0,1:T(8,128)S(1)} %get-tuple-element.995), channel_id=1, source_target_pairs={{3,0},{4,1},{5,2},{6,3},{7,4},{8,5},{9,6},{10,7},{11,8},{12,9},{13... | collective-permute-start | bytes 98312 | tf_op jit(solution)/shard_map/ppermute | solution.py:18
  164.9 69.7 %copy-start.4 = (f32[32,1024]{0,1:T(8,128)}, f32[32,1024]{0,1:T(8,128)S(1)}, u32[]{:S(2)}) copy-start(f32[32,1024]{0,1:T(8,128)S(1)} %get-tuple-element.983) | copy-start | bytes 393220
  166.2 17.4 %collective-permute-start.6 = (f32[32,128]{1,0:T(8,128)S(1)}, f32[32,128]{1,0:T(8,128)S(1)}, u32[]{:S(2)}, u32[]{:S(2)}) collective-permute-start(f32[32,128]{1,0:T(8,128)S(1)} %bitcast.328), channel_id=1, source_target_pairs={{63,0},{0,1},{1,2},{2,3},{3,4},{4,5},{5,6},{6,7},{7,8},{8,9},{9,10... | collective-permute-start | bytes 49160 | tf_op jit(solution)/shard_map/ppermute | solution.py:18
  169.6 19.9 %collective-permute-start.7 = (f32[32,128]{1,0:T(8,128)S(1)}, f32[32,128]{1,0:T(8,128)S(1)}, u32[]{:S(2)}, u32[]{:S(2)}) collective-permute-start(f32[32,128]{1,0:T(8,128)S(1)} %bitcast.324), channel_id=1, source_target_pairs={{1,0},{2,1},{3,2},{4,3},{5,4},{6,5},{7,6},{8,7},{9,8},{10,9},{11,1... | collective-permute-start | bytes 49160 | tf_op jit(solution)/shard_map/ppermute | solution.py:18
  173.3 16.8 %collective-permute-start.8 = (f32[32,128]{1,0:T(8,128)S(1)}, f32[32,128]{1,0:T(8,128)S(1)}, u32[]{:S(2)}, u32[]{:S(2)}) collective-permute-start(f32[32,128]{1,0:T(8,128)S(1)} %bitcast.320), channel_id=1, source_target_pairs={{62,0},{63,1},{0,2},{1,3},{2,4},{3,5},{4,6},{5,7},{6,8},{7,9},{8,1... | collective-permute-start | bytes 49160 | tf_op jit(solution)/shard_map/ppermute | solution.py:18
  173.3 17.4 %collective-permute-start.9 = (f32[32,128]{1,0:T(8,128)S(1)}, f32[32,128]{1,0:T(8,128)S(1)}, u32[]{:S(2)}, u32[]{:S(2)}) collective-permute-start(f32[32,128]{1,0:T(8,128)S(1)} %bitcast.316), channel_id=1, source_target_pairs={{2,0},{3,1},{4,2},{5,3},{6,4},{7,5},{8,6},{9,7},{10,8},{11,9},{12,... | collective-permute-start | bytes 49160 | tf_op jit(solution)/shard_map/ppermute | solution.py:18
  178.1 13.2 %collective-permute-start.10 = (f32[32,128]{1,0:T(8,128)S(1)}, f32[32,128]{1,0:T(8,128)S(1)}, u32[]{:S(2)}, u32[]{:S(2)}) collective-permute-start(f32[32,128]{1,0:T(8,128)S(1)} %bitcast.312), channel_id=1, source_target_pairs={{61,0},{62,1},{63,2},{0,3},{1,4},{2,5},{3,6},{4,7},{5,8},{6,9},{7,... | collective-permute-start | bytes 49160 | tf_op jit(solution)/shard_map/ppermute | solution.py:18
  183.6 8.3 %collective-permute-start.11 = (f32[32,128]{1,0:T(8,128)S(1)}, f32[32,128]{1,0:T(8,128)S(1)}, u32[]{:S(2)}, u32[]{:S(2)}) collective-permute-start(f32[32,128]{1,0:T(8,128)S(1)} %bitcast.308), channel_id=1, source_target_pairs={{3,0},{4,1},{5,2},{6,3},{7,4},{8,5},{9,6},{10,7},{11,8},{12,9},{13... | collective-permute-start | bytes 49160 | tf_op jit(solution)/shard_map/ppermute | solution.py:18
  193.2 18.2 %copy-start.13 = (f32[8,384]{1,0:T(8,128)S(1)}, f32[8,384]{1,0:T(8,128)}, u32[]{:S(2)}) copy-start(f32[8,384]{1,0:T(8,128)} %mul.242) | copy-start | bytes 36868
  227.7 6.9 %copy-start.9 = (f32[32,1024]{0,1:T(8,128)S(1)}, f32[32,1024]{0,1:T(8,128)}, u32[]{:S(2)}) copy-start(f32[32,1024]{0,1:T(8,128)} %copy.443) | copy-start | bytes 393220
  236.4 17.1 %collective-permute-start.12 = (f32[32,128]{1,0:T(8,128)S(1)}, f32[32,128]{1,0:T(8,128)S(1)}, u32[]{:S(2)}, u32[]{:S(2)}) collective-permute-start(f32[32,128]{1,0:T(8,128)S(1)} %bitcast.329), channel_id=1, source_target_pairs={{63,0},{0,1},{1,2},{2,3},{3,4},{4,5},{5,6},{6,7},{7,8},{8,9},{9,10... | collective-permute-start | bytes 49160 | tf_op jit(solution)/shard_map/ppermute | solution.py:18
  239.3 19.4 %collective-permute-start.13 = (f32[32,128]{1,0:T(8,128)S(1)}, f32[32,128]{1,0:T(8,128)S(1)}, u32[]{:S(2)}, u32[]{:S(2)}) collective-permute-start(f32[32,128]{1,0:T(8,128)S(1)} %bitcast.325), channel_id=1, source_target_pairs={{1,0},{2,1},{3,2},{4,3},{5,4},{6,5},{7,6},{8,7},{9,8},{10,9},{11,1... | collective-permute-start | bytes 49160 | tf_op jit(solution)/shard_map/ppermute | solution.py:18
  243.1 15.6 %collective-permute-start.14 = (f32[32,128]{1,0:T(8,128)S(1)}, f32[32,128]{1,0:T(8,128)S(1)}, u32[]{:S(2)}, u32[]{:S(2)}) collective-permute-start(f32[32,128]{1,0:T(8,128)S(1)} %bitcast.321), channel_id=1, source_target_pairs={{62,0},{63,1},{0,2},{1,3},{2,4},{3,5},{4,6},{5,7},{6,8},{7,9},{8,1... | collective-permute-start | bytes 49160 | tf_op jit(solution)/shard_map/ppermute | solution.py:18
  243.1 15.6 %collective-permute-start.15 = (f32[32,128]{1,0:T(8,128)S(1)}, f32[32,128]{1,0:T(8,128)S(1)}, u32[]{:S(2)}, u32[]{:S(2)}) collective-permute-start(f32[32,128]{1,0:T(8,128)S(1)} %bitcast.317), channel_id=1, source_target_pairs={{2,0},{3,1},{4,2},{5,3},{6,4},{7,5},{8,6},{9,7},{10,8},{11,9},{12,... | collective-permute-start | bytes 49160 | tf_op jit(solution)/shard_map/ppermute | solution.py:18
  248.0 10.8 %collective-permute-start.16 = (f32[32,128]{1,0:T(8,128)S(1)}, f32[32,128]{1,0:T(8,128)S(1)}, u32[]{:S(2)}, u32[]{:S(2)}) collective-permute-start(f32[32,128]{1,0:T(8,128)S(1)} %bitcast.313), channel_id=1, source_target_pairs={{61,0},{62,1},{63,2},{0,3},{1,4},{2,5},{3,6},{4,7},{5,8},{6,9},{7,... | collective-permute-start | bytes 49160 | tf_op jit(solution)/shard_map/ppermute | solution.py:18
  253.5 6.0 %collective-permute-start.17 = (f32[32,128]{1,0:T(8,128)S(1)}, f32[32,128]{1,0:T(8,128)S(1)}, u32[]{:S(2)}, u32[]{:S(2)}) collective-permute-start(f32[32,128]{1,0:T(8,128)S(1)} %bitcast.309), channel_id=1, source_target_pairs={{3,0},{4,1},{5,2},{6,3},{7,4},{8,5},{9,6},{10,7},{11,8},{12,9},{13... | collective-permute-start | bytes 49160 | tf_op jit(solution)/shard_map/ppermute | solution.py:18
  286.6 7.0 %copy-start.5 = (f32[32,1024]{0,1:T(8,128)S(1)}, f32[32,1024]{0,1:T(8,128)}, u32[]{:S(2)}) copy-start(f32[32,1024]{0,1:T(8,128)} %copy-done.4) | copy-start | bytes 393220
  286.6 7.0 %copy-start.7 = (f32[32,1024]{0,1:T(8,128)S(1)}, f32[32,1024]{0,1:T(8,128)}, u32[]{:S(2)}) copy-start(f32[32,1024]{0,1:T(8,128)} %copy.447) | copy-start | bytes 393220
  286.6 7.0 %copy-start.27 = (f32[1024]{0:T(1024)S(1)}, f32[1024]{0:T(1024)}, u32[]{:S(2)}) copy-start(f32[1024]{0:T(1024)} %get-tuple-element.1028) | copy-start | bytes 12292
  294.5 138.7 %copy-start = (f32[32,1024]{0,1:T(8,128)}, f32[32,1024]{0,1:T(8,128)S(1)}, u32[]{:S(2)}) copy-start(f32[32,1024]{0,1:T(8,128)S(1)} %get-tuple-element.981) | copy-start | bytes 393220
  295.8 24.2 %all-to-all-start = ((f32[64,1,33]{2,1,0:T(1,128)}), f32[64,1,33]{2,1,0:T(1,128)S(1)}, u32[]{:S(2)}, u32[]{:S(2)}) async-start(f32[64,1,33]{2,1,0:T(1,128)} %broadcast_in_dim.164), calls=%async_computation | async-start | bytes 65536 | tf_op jit(solution)/shard_map/all_to_all | solution.py:23
  324.9 13.0 %collective-permute-start.18 = (f32[64,128]{0,1:T(8,128)S(1)}, f32[64,128]{0,1:T(8,128)S(1)}, u32[]{:S(2)}, u32[]{:S(2)}) collective-permute-start(f32[64,128]{0,1:T(8,128)S(1)} %get-tuple-element.994), channel_id=1, source_target_pairs={{63,0},{0,1},{1,2},{2,3},{3,4},{4,5},{5,6},{6,7},{7,8},{8,9},{9,10... | collective-permute-start | bytes 98312 | tf_op jit(solution)/shard_map/ppermute | solution.py:18
  327.5 16.0 %collective-permute-start.19 = (f32[64,128]{0,1:T(8,128)S(1)}, f32[64,128]{0,1:T(8,128)S(1)}, u32[]{:S(2)}, u32[]{:S(2)}) collective-permute-start(f32[64,128]{0,1:T(8,128)S(1)} %get-tuple-element.993), channel_id=1, source_target_pairs={{1,0},{2,1},{3,2},{4,3},{5,4},{6,5},{7,6},{8,7},{9,8},{10,9},{11,1... | collective-permute-start | bytes 98312 | tf_op jit(solution)/shard_map/ppermute | solution.py:18
  327.5 16.6 %collective-permute-start.20 = (f32[64,128]{0,1:T(8,128)S(1)}, f32[64,128]{0,1:T(8,128)S(1)}, u32[]{:S(2)}, u32[]{:S(2)}) collective-permute-start(f32[64,128]{0,1:T(8,128)S(1)} %get-tuple-element.992), channel_id=1, source_target_pairs={{62,0},{63,1},{0,2},{1,3},{2,4},{3,5},{4,6},{5,7},{6,8},{7,9},{8,1... | collective-permute-start | bytes 98312 | tf_op jit(solution)/shard_map/ppermute | solution.py:18
  328.7 16.1 %collective-permute-start.21 = (f32[64,128]{0,1:T(8,128)S(1)}, f32[64,128]{0,1:T(8,128)S(1)}, u32[]{:S(2)}, u32[]{:S(2)}) collective-permute-start(f32[64,128]{0,1:T(8,128)S(1)} %get-tuple-element.991), channel_id=1, source_target_pairs={{2,0},{3,1},{4,2},{5,3},{6,4},{7,5},{8,6},{9,7},{10,8},{11,9},{12,... | collective-permute-start | bytes 98312 | tf_op jit(solution)/shard_map/ppermute | solution.py:18
  332.3 13.1 %collective-permute-start.22 = (f32[64,128]{0,1:T(8,128)S(1)}, f32[64,128]{0,1:T(8,128)S(1)}, u32[]{:S(2)}, u32[]{:S(2)}) collective-permute-start(f32[64,128]{0,1:T(8,128)S(1)} %get-tuple-element.990), channel_id=1, source_target_pairs={{61,0},{62,1},{63,2},{0,3},{1,4},{2,5},{3,6},{4,7},{5,8},{6,9},{7,... | collective-permute-start | bytes 98312 | tf_op jit(solution)/shard_map/ppermute | solution.py:18
  334.0 12.6 %copy-start.44 = (f32[64,1]{0,1:T(1,128)S(1)}, f32[64,1]{0,1:T(1,128)}, u32[]{:S(2)}) copy-start(f32[64,1]{0,1:T(1,128)} %copy-done.43) | copy-start | bytes 772
  337.8 8.2 %collective-permute-start.23 = (f32[64,128]{0,1:T(8,128)S(1)}, f32[64,128]{0,1:T(8,128)S(1)}, u32[]{:S(2)}, u32[]{:S(2)}) collective-permute-start(f32[64,128]{0,1:T(8,128)S(1)} %get-tuple-element.989), channel_id=1, source_target_pairs={{3,0},{4,1},{5,2},{6,3},{7,4},{8,5},{9,6},{10,7},{11,8},{12,9},{13... | collective-permute-start | bytes 98312 | tf_op jit(solution)/shard_map/ppermute | solution.py:18
  353.2 17.1 %copy-start.12 = (f32[32,3072]{1,0:T(8,128)S(1)}, f32[32,3072]{1,0:T(8,128)}, u32[]{:S(2)}) copy-start(f32[32,3072]{1,0:T(8,128)} %param.48) | copy-start | bytes 1179652
  353.2 17.1 %copy-start.25 = (f32[3072]{0:T(1024)S(1)}, f32[3072]{0:T(1024)}, u32[]{:S(2)}) copy-start(f32[3072]{0:T(1024)} %param.49) | copy-start | bytes 36868
  394.7 10.8 %copy-start.14 = (f32[8,384]{1,0:T(8,128)S(1)}, f32[8,384]{1,0:T(8,128)}, u32[]{:S(2)}) copy-start(f32[8,384]{1,0:T(8,128)} %mul.242) | copy-start | bytes 36868
  438.0 13.3 %collective-permute-start.24 = (f32[32,128]{1,0:T(8,128)S(1)}, f32[32,128]{1,0:T(8,128)}, u32[]{:S(2)}, u32[]{:S(2)}) collective-permute-start(f32[32,128]{1,0:T(8,128)S(1)} %bitcast.330), channel_id=1, source_target_pairs={{63,0},{0,1},{1,2},{2,3},{3,4},{4,5},{5,6},{6,7},{7,8},{8,9},{9,10... | collective-permute-start | bytes 49160 | tf_op jit(solution)/shard_map/ppermute | solution.py:18
  440.8 16.5 %collective-permute-start.25 = (f32[32,128]{1,0:T(8,128)S(1)}, f32[32,128]{1,0:T(8,128)}, u32[]{:S(2)}, u32[]{:S(2)}) collective-permute-start(f32[32,128]{1,0:T(8,128)S(1)} %bitcast.326), channel_id=1, source_target_pairs={{1,0},{2,1},{3,2},{4,3},{5,4},{6,5},{7,6},{8,7},{9,8},{10,9},{11,1... | collective-permute-start | bytes 49160 | tf_op jit(solution)/shard_map/ppermute | solution.py:18
  444.6 13.5 %collective-permute-start.26 = (f32[32,128]{1,0:T(8,128)S(1)}, f32[32,128]{1,0:T(8,128)}, u32[]{:S(2)}, u32[]{:S(2)}) collective-permute-start(f32[32,128]{1,0:T(8,128)S(1)} %bitcast.322), channel_id=1, source_target_pairs={{62,0},{63,1},{0,2},{1,3},{2,4},{3,5},{4,6},{5,7},{6,8},{7,9},{8,1... | collective-permute-start | bytes 49160 | tf_op jit(solution)/shard_map/ppermute | solution.py:18
  444.6 14.2 %collective-permute-start.27 = (f32[32,128]{1,0:T(8,128)S(1)}, f32[32,128]{1,0:T(8,128)S(1)}, u32[]{:S(2)}, u32[]{:S(2)}) collective-permute-start(f32[32,128]{1,0:T(8,128)S(1)} %bitcast.318), channel_id=1, source_target_pairs={{2,0},{3,1},{4,2},{5,3},{6,4},{7,5},{8,6},{9,7},{10,8},{11,9},{12,... | collective-permute-start | bytes 49160 | tf_op jit(solution)/shard_map/ppermute | solution.py:18
  449.4 9.4 %collective-permute-start.28 = (f32[32,128]{1,0:T(8,128)S(1)}, f32[32,128]{1,0:T(8,128)S(1)}, u32[]{:S(2)}, u32[]{:S(2)}) collective-permute-start(f32[32,128]{1,0:T(8,128)S(1)} %bitcast.314), channel_id=1, source_target_pairs={{61,0},{62,1},{63,2},{0,3},{1,4},{2,5},{3,6},{4,7},{5,8},{6,9},{7,... | collective-permute-start | bytes 49160 | tf_op jit(solution)/shard_map/ppermute | solution.py:18
  449.7 6.9 %copy-start.24 = (f32[32,1793]{1,0:T(8,128)S(1)}, f32[32,1793]{1,0:T(8,128)}, u32[]{:S(2)}) copy-start(f32[32,1793]{1,0:T(8,128)} %constant_dynamic-update-slice_fusion.35) | copy-start | bytes 688516
  451.4 7.4 %collective-permute-start.29 = (f32[32,128]{1,0:T(8,128)S(1)}, f32[32,128]{1,0:T(8,128)S(1)}, u32[]{:S(2)}, u32[]{:S(2)}) collective-permute-start(f32[32,128]{1,0:T(8,128)S(1)} %bitcast.310), channel_id=1, source_target_pairs={{3,0},{4,1},{5,2},{6,3},{7,4},{8,5},{9,6},{10,7},{11,8},{12,9},{13... | collective-permute-start | bytes 49160 | tf_op jit(solution)/shard_map/ppermute | solution.py:18
  482.3 7.0 %copy-start.1 = (f32[32,1024]{0,1:T(8,128)S(1)}, f32[32,1024]{0,1:T(8,128)}, u32[]{:S(2)}) copy-start(f32[32,1024]{0,1:T(8,128)} %copy-done) | copy-start | bytes 393220
  482.3 7.0 %copy-start.2 = (f32[32,1024]{0,1:T(8,128)S(1)}, f32[32,1024]{0,1:T(8,128)}, u32[]{:S(2)}) copy-start(f32[32,1024]{0,1:T(8,128)} %get-tuple-element.976) | copy-start | bytes 393220
  482.3 7.0 %copy-start.8 = (f32[32,1024]{0,1:T(8,128)S(1)}, f32[32,1024]{0,1:T(8,128)}, u32[]{:S(2)}) copy-start(f32[32,1024]{0,1:T(8,128)} %copy.469) | copy-start | bytes 393220
  482.3 7.0 %copy-start.35 = (f32[32]{0:T(128)S(1)}, f32[32]{0:T(128)}, u32[]{:S(2)}) copy-start(f32[32]{0:T(128)} %copy-done.33) | copy-start | bytes 388
  491.0 17.1 %collective-permute-start.30 = (f32[32,128]{1,0:T(8,128)S(1)}, f32[32,128]{1,0:T(8,128)S(1)}, u32[]{:S(2)}, u32[]{:S(2)}) collective-permute-start(f32[32,128]{1,0:T(8,128)S(1)} %bitcast.331), channel_id=1, source_target_pairs={{63,0},{0,1},{1,2},{2,3},{3,4},{4,5},{5,6},{6,7},{7,8},{8,9},{9,10... | collective-permute-start | bytes 49160 | tf_op jit(solution)/shard_map/ppermute | solution.py:18
  494.0 19.4 %collective-permute-start.31 = (f32[32,128]{1,0:T(8,128)S(1)}, f32[32,128]{1,0:T(8,128)S(1)}, u32[]{:S(2)}, u32[]{:S(2)}) collective-permute-start(f32[32,128]{1,0:T(8,128)S(1)} %bitcast.327), channel_id=1, source_target_pairs={{1,0},{2,1},{3,2},{4,3},{5,4},{6,5},{7,6},{8,7},{9,8},{10,9},{11,1... | collective-permute-start | bytes 49160 | tf_op jit(solution)/shard_map/ppermute | solution.py:18
  497.8 15.5 %collective-permute-start.32 = (f32[32,128]{1,0:T(8,128)S(1)}, f32[32,128]{1,0:T(8,128)S(1)}, u32[]{:S(2)}, u32[]{:S(2)}) collective-permute-start(f32[32,128]{1,0:T(8,128)S(1)} %bitcast.323), channel_id=1, source_target_pairs={{62,0},{63,1},{0,2},{1,3},{2,4},{3,5},{4,6},{5,7},{6,8},{7,9},{8,1... | collective-permute-start | bytes 49160 | tf_op jit(solution)/shard_map/ppermute | solution.py:18
  497.8 15.6 %collective-permute-start.33 = (f32[32,128]{1,0:T(8,128)S(1)}, f32[32,128]{1,0:T(8,128)S(1)}, u32[]{:S(2)}, u32[]{:S(2)}) collective-permute-start(f32[32,128]{1,0:T(8,128)S(1)} %bitcast.319), channel_id=1, source_target_pairs={{2,0},{3,1},{4,2},{5,3},{6,4},{7,5},{8,6},{9,7},{10,8},{11,9},{12,... | collective-permute-start | bytes 49160 | tf_op jit(solution)/shard_map/ppermute | solution.py:18
  502.6 10.8 %collective-permute-start.34 = (f32[32,128]{1,0:T(8,128)S(1)}, f32[32,128]{1,0:T(8,128)S(1)}, u32[]{:S(2)}, u32[]{:S(2)}) collective-permute-start(f32[32,128]{1,0:T(8,128)S(1)} %bitcast.315), channel_id=1, source_target_pairs={{61,0},{62,1},{63,2},{0,3},{1,4},{2,5},{3,6},{4,7},{5,8},{6,9},{7,... | collective-permute-start | bytes 49160 | tf_op jit(solution)/shard_map/ppermute | solution.py:18
  508.2 6.0 %collective-permute-start.35 = (f32[32,128]{1,0:T(8,128)S(1)}, f32[32,128]{1,0:T(8,128)S(1)}, u32[]{:S(2)}, u32[]{:S(2)}) collective-permute-start(f32[32,128]{1,0:T(8,128)S(1)} %bitcast.311), channel_id=1, source_target_pairs={{3,0},{4,1},{5,2},{6,3},{7,4},{8,5},{9,6},{10,7},{11,8},{12,9},{13... | collective-permute-start | bytes 49160 | tf_op jit(solution)/shard_map/ppermute | solution.py:18
  555.2 7.0 %copy-start.3 = (f32[32,1024]{0,1:T(8,128)S(1)}, f32[32,1024]{0,1:T(8,128)}, u32[]{:S(2)}) copy-start(f32[32,1024]{0,1:T(8,128)} %get-tuple-element.976) | copy-start | bytes 393220
  555.2 7.0 %copy-start.6 = (f32[32,1024]{0,1:T(8,128)S(1)}, f32[32,1024]{0,1:T(8,128)}, u32[]{:S(2)}) copy-start(f32[32,1024]{0,1:T(8,128)} %copy.473) | copy-start | bytes 393220
  555.2 7.0 %copy-start.23 = (pred[1024]{0:T(1024)(128)(4,1)S(1)}, pred[1024]{0:T(1024)(128)(4,1)}, u32[]{:S(2)}) copy-start(pred[1024]{0:T(1024)(128)(4,1)} %iota_compare_fusion.87) | copy-start | bytes 3076
  555.2 7.0 %copy-start.28 = (f32[1024]{0:T(1024)S(1)}, f32[1024]{0:T(1024)}, u32[]{:S(2)}) copy-start(f32[1024]{0:T(1024)} %get-tuple-element.1028) | copy-start | bytes 12292
  563.1 31.1 %copy-start.11 = (f32[32,1024]{0,1:T(8,128)S(1)}, f32[32,1024]{0,1:T(8,128)}, u32[]{:S(2)}) copy-start(f32[32,1024]{0,1:T(8,128)} %get-tuple-element.977) | copy-start | bytes 393220
  590.2 12.3 %all-to-all-start.2 = ((f32[4,32,1024]{2,1,0:T(8,128)}), f32[4,32,1024]{2,1,0:T(8,128)S(1)}, u32[]{:S(2)}, u32[]{:S(2)}) async-start(f32[4,32,1024]{2,1,0:T(8,128)} %broadcast_in_dim.172), calls=%async_computation.2 | async-start | bytes 1048576 | tf_op jit(solution)/shard_map/all_to_all | solution.py:23
  (19 other events, 66.4 us)
where the time goes:
time: 616 us; the launch traced here: 604 us
  matrix products  185 us (30%)
  local copies, waits for them, and re-layouts  177 us (29%)
  starting transfers between devices  111 us (18%)
  other arithmetic  92.7 us (15%)
  blocking collectives  23.8 us (4%)
  waiting for transfers between devices  8.2 us (1%)
    dot_general x132, matrix products, exact_dot(): jnp.dot(left_side, right_side, precision=lax.Precision.HIGHEST, preferred...  179 us
    ppermute x36, starting transfers between devices, passed_along(): return lax.ppermute(block, axis, route)  92.1 us
    reduce_sum x8, other arithmetic, divergence(): outgoing = jnp.sum(fluxes.reshape(levels, cell_count, 3), axis=2)  50.5 us
    unnamed x144, local copies, waits for them, and re-layouts  38.6 us
    reshape x10, local copies, waits for them, and re-layouts, starts_of(): jnp.broadcast_to(fields[:, :, None], (levels, cell_count, 3))  31.1 us
    all_to_all x1, blocking collectives, from_everyone(): return lax.all_to_all(copies, axis, split_axis=0, concat_axis=0, tiled=True)  23.8 us
    transpose x6, other arithmetic, divergence(): jnp.transpose(fluxes.reshape(levels, block_count, block_size), (1, 0, 2))  19.8 us
    all_to_all x2, starting transfers between devices, from_everyone(): return lax.all_to_all(copies, axis, split_axis=0, concat_axis=0, tiled=True)  19 us
  transfers between devices with their start and end apart: 38, of which 4 were waited for; matrix products, arithmetic and copies ran while one was open for 12% of the time, Pallas kernels for 0%

commit v1 on v0

v1 whole, which is shorter than its diff:
```python
import jax
import jax.numpy as jnp
from jax import lax
from jax.experimental import pallas as pl
from jax.experimental.pallas import tpu as pltpu
from jax.sharding import PartitionSpec as P

MESH = pl.DeviceIdType.MESH
F32 = jnp.float32
BF16 = jnp.bfloat16

LV = 32
CC = 1024
NBK = 6
HB = 128
HALO = NBK * HB
EXT = CC + HALO
LINE = 16
DT = 0.25
NS = 3
OFFSETS = [(b // 2 + 1) * (1 - 2 * (b % 2)) for b in range(NBK)]
GRID = 1024.0


def split2(x):
    hi = x.astype(BF16)
    lo = (x - hi.astype(F32)).astype(BF16)
    return hi, lo


def rows2(x):
    return jnp.concatenate(split2(x), axis=0)


def split3(x):
    a = x.astype(BF16)
    r = x - a.astype(F32)
    b = r.astype(BF16)
    c = (r - b.astype(F32)).astype(BF16)
    return a, b, c


def mm(a, b):
    return jnp.dot(a, b, preferred_element_type=F32)


def mm_t(a, b):
    return lax.dot_general(a, b, (((1,), (1,)), ((), ())), preferred_element_type=F32)


def fold(o):
    return o[:LV] + o[LV : 2 * LV]


def kernel(
    par, tot, p_in, q_in, t_in, v_in, small_in, inv_in, exp_in, end_in,
    p_out, t_out, e_out,
    sel, mat, esel, vd, sd, snd, rcv, row_a, row_b, row_m, box_a, box_b, box_m,
    cur_buf, rs_box, slab, ens, s_send, s_recv, a_send, a_recv, x_send, x_recv,
):
    n_mem = lax.axis_size("member")
    n_dom = lax.axis_size("dom")
    n_line = n_dom // LINE
    m = lax.axis_index("member")
    d = lax.axis_index("dom")
    line, pos = d // LINE, d % LINE

    neighbours = [(m, (d + off + n_dom) % n_dom) for off in OFFSETS]
    in_line = [(m, line * LINE + (pos + k) % LINE) for k in range(1, LINE)]
    across = [(m, (d + k * LINE) % n_dom) for k in range(1, n_line)]
    members = [((m + k) % n_mem, d) for k in range(1, n_mem)]

    barrier = pltpu.get_barrier_semaphore()
    peers = neighbours + in_line + across + members
    for peer in peers:
        pl.semaphore_signal(barrier, inc=1, device_id=peer, device_id_type=MESH)

    speed = par[0, 0]
    kappa = 0.5 * par[0, 1]
    mixing = 0.6 * par[0, 2]
    couple = par[0, 3]
    owned = lax.broadcasted_iota(jnp.int32, (1, CC), 1) < tot[0]
    inv = inv_in[...]
    iota16 = lax.broadcasted_iota(jnp.int32, (16, HB), 0).astype(F32).astype(BF16)
    one = jnp.full((16, HB), 1.0, BF16)
    zero = jnp.full((16, HB), 0.0, BF16)

    def packed_row(row):
        return jnp.broadcast_to(row, (16, HB)).astype(BF16)

    def build_exports(t, carry):
        base = pl.multiple_of(t * 256, 256)
        for b in range(NBK):
            want = exp_in[0, b : b + 1, :].astype(F32) - (t * 256).astype(F32)
            want = packed_row(jnp.clip(want, -1.0, 256.0))
            for r in range(16):
                hit = (iota16 + jnp.asarray(16.0 * r, BF16)) == want
                esel[pl.ds(base + 16 * r, 16), b * HB : (b + 1) * HB] = jnp.where(hit, one, zero)
        return carry

    lax.fori_loop(0, CC // 256, build_exports, 0)

    def store_rows(slot, values):
        for b in range(NBK):
            snd[slot, b] = values[:, b * HB : (b + 1) * HB]

    def halo_copy(slot, b):
        return pltpu.make_async_remote_copy(
            src_ref=snd.at[slot, b],
            dst_ref=rcv.at[slot, b],
            send_sem=s_send.at[slot, b],
            recv_sem=s_recv.at[slot, b],
            device_id=neighbours[b],
            device_id_type=MESH,
        )

    def send(slot):
        for b in range(NBK):
            halo_copy(slot, b).start()

    def receive(slot):
        for b in range(NBK):
            halo_copy(slot, b).wait_recv()
        return jnp.concatenate([rcv[slot, b] for b in range(NBK)], axis=1)

    pres = p_in[0]
    prev = q_in[0]
    theta = t_in[0]
    both = mm(jnp.concatenate([rows2(theta), rows2(pres)], axis=0), esel[...])
    store_rows(6, fold(both[: 2 * LV]))
    store_rows(0, fold(both[2 * LV :]))
    pl.semaphore_wait(barrier, len(peers))
    send(6)
    send(0)

    er = lax.broadcasted_iota(jnp.int32, (3 * HB, 3 * HB), 0)
    ec = lax.broadcasted_iota(jnp.int32, (3 * HB, 3 * HB), 1)
    order = jnp.where(er == 3 * (ec % HB) + ec // HB, 1.0, 0.0).astype(F32).astype(BF16)
    ends = end_in[1:2, :]
    end_hi = (ends // 256).astype(F32)
    end_lo = (ends % 256).astype(F32)
    smalls = jnp.concatenate([end_hi, end_lo, small_in[...], jnp.zeros((4, 3 * CC), F32)], axis=0)
    s1, s2, s3 = split3(smalls)
    v1, v2, v3 = split3(v_in[...])
    stacked = jnp.concatenate([v1, v2, v3], axis=0)
    stacked_small = jnp.concatenate([s1.astype(F32), s2.astype(F32), s3.astype(F32)], axis=0)
    stacked_small = jnp.concatenate([stacked_small, jnp.zeros((8, 3 * CC), F32)], axis=0).astype(BF16)
    for g in range(CC // HB):
        cols = slice(g * 3 * HB, (g + 1) * 3 * HB)
        o = mm(jnp.concatenate([stacked[:, cols], stacked_small[:, cols]], axis=0), order)
        vel = o[:LV] + o[LV : 2 * LV] + o[2 * LV : 3 * LV]
        small = o[96:104] + o[104:112] + o[112:120]
        for j in range(3):
            vd[j, :, g * HB : (g + 1) * HB] = vel[:, j * HB : (j + 1) * HB]
            sd[j, :, g * HB : (g + 1) * HB] = small[:, j * HB : (j + 1) * HB]

    def build(t, carry):
        base = pl.multiple_of(t * 256, 256)
        tf = t.astype(F32)
        for g in range(CC // HB):
            lanes = slice(g * HB, (g + 1) * HB)
            want, whi, wlo = [], [], []
            for j in range(3):
                offset = (sd[j, 0:1, lanes] - tf) * 256.0 + sd[j, 1:2, lanes]
                want.append(packed_row(jnp.clip(offset, -1.0, 256.0)))
                w = sd[j, 3:4, lanes]
                lead = jnp.floor(w * GRID + 0.5) * (1.0 / GRID)
                whi.append(packed_row(lead))
                wlo.append(packed_row(w - lead))
            for r in range(16):
                row = pl.ds(base + 16 * r, 16)
                place = iota16 + jnp.asarray(16.0 * r, BF16)
                hit = [place == want[j] for j in range(3)]
                for j in range(3):
                    sel[j, row, lanes] = jnp.where(hit[j], one, zero)
                hi = [jnp.where(hit[j], whi[j], zero) for j in range(3)]
                lo = [jnp.where(hit[j], wlo[j], zero) for j in range(3)]
                mat[0, row, lanes] = hi[0] + hi[1] + hi[2]
                mat[1, row, lanes] = lo[0] + lo[1] + lo[2]
        return carry

    lax.fori_loop(0, EXT // 256, build, 0)

    def coefficients(j):
        v = vd[j]
        length = sd[j, 2:3, :]
        return length * (jnp.maximum(v, 0.0) + kappa), length * (jnp.minimum(v, 0.0) - kappa)

    def theta_local(th):
        lhs = rows2(th)
        net = jnp.zeros((LV, CC), F32)
        for j in range(3):
            near, far = coefficients(j)
            flux = near * th + far * fold(mm(lhs, sel[j, :CC, :]))
            net = net + flux - fold(mm_t(rows2(flux), sel[j, :CC, :]))
        return net

    def theta_finish(th, net, halo):
        lhs = rows2(halo)
        for j in range(3):
            net = net + coefficients(j)[1] * fold(mm(lhs, sel[j, CC:, :]))
        up = jnp.concatenate([th[1:], th[LV - 1 :]], axis=0) - th
        down = th - jnp.concatenate([th[:1], th[: LV - 1]], axis=0)
        return jnp.where(owned, th + DT * (mixing * (up - down) - inv * net), th)

    ones = jnp.ones((16, CC), BF16)

    def local_rows(p, with_ones=False):
        lhs = rows2(p)
        if with_ones:
            lhs = jnp.concatenate([lhs, ones], axis=0)
        return (
            mm(lhs, mat[0, :CC, :]) + mm(lhs, mat[1, :CC, :])
            + mm_t(lhs, mat[0, :CC, :]) + mm_t(lhs, mat[1, :CC, :])
        )

    def halo_rows(h, with_ones=False):
        lhs = rows2(h)
        if with_ones:
            lhs = jnp.concatenate([lhs, ones[:, :HALO]], axis=0)
        return mm(lhs, mat[0, CC:, :]) + mm(lhs, mat[1, CC:, :])

    scale = speed * inv

    def advance(p, q, near, far, degree, force):
        change = scale * (fold(near) + fold(far) - degree * p) + force
        return jnp.where(owned, 2.0 * p - q + change, p), p

    def export(p):
        return fold(mm(rows2(p), esel[...]))

    area = jnp.where(owned, 1.0 / inv, 0.0)

    def partial_row(p):
        total = jnp.zeros((LV, HB), F32)
        spread = jnp.zeros((1, HB), F32)
        for g in range(CC // HB):
            lanes = slice(g * HB, (g + 1) * HB)
            total = total + p[:, lanes] * area[:, lanes]
            spread = spread + area[:, lanes]
        padded = jnp.concatenate([total, spread, jnp.zeros((HB - LV - 1, HB), F32)], axis=0)
        return jnp.sum(padded.T, axis=0, keepdims=True)

    def spread_row(row):
        return jnp.broadcast_to(row, (HB, HB)).T[:LV]

    def line_copy(which, k):
        return pltpu.make_async_remote_copy(
            src_ref=row_a.at[which],
            dst_ref=box_a.at[which, pos],
            send_sem=a_send.at[which, k],
            recv_sem=a_recv.at[which, k],
            device_id=in_line[k - 1],
            device_id_type=MESH,
        )

    def across_copy(which, k):
        return pltpu.make_async_remote_copy(
            src_ref=row_b.at[which],
            dst_ref=box_b.at[which, line],
            send_sem=a_send.at[which, LINE + k],
            recv_sem=a_recv.at[which, LINE + k],
            device_id=across[k - 1],
            device_id_type=MESH,
        )

    def start_mean(which, p):
        row = partial_row(p)
        row_a[which] = row
        box_a[which, pos] = row
        for k in range(1, LINE):
            line_copy(which, k).start()

    def turn_mean(which):
        for k in range(1, LINE):
            line_copy(which, k).wait_recv()
        row = jnp.sum(box_a[which], axis=0)
        row_b[which] = row
        box_b[which, line] = row
        for k in range(1, n_line):
            across_copy(which, k).start()

    def end_mean(which):
        for k in range(1, n_line):
            across_copy(which, k).wait_recv()
        row = jnp.sum(box_b[which], axis=0)
        return row / row[:, LV : LV + 1]

    def less_mean(p, level_mean):
        wide = jnp.concatenate([level_mean] * (CC // HB), axis=1)
        return p - jnp.where(owned, wide, 0.0)

    net = theta_local(theta)
    near = local_rows(pres, True)
    theta_next = theta_finish(theta, net, receive(6))
    force = couple * (theta_next - theta) / NS
    theta = theta_next
    far = halo_rows(receive(0), True)
    degree = near[2 * LV : 2 * LV + 1] + far[2 * LV : 2 * LV + 1]
    pres, prev = advance(pres, prev, near, far, degree, force)
    store_rows(1, export(pres))
    send(1)
    store_rows(7, export(theta))
    send(7)
    near = local_rows(pres)
    pres, prev = advance(pres, prev, near, halo_rows(receive(1)), degree, force)
    store_rows(2, export(pres))
    send(2)
    near = local_rows(pres)
    net = theta_local(theta)
    pres, prev = advance(pres, prev, near, halo_rows(receive(2)), degree, force)
    store_rows(3, export(pres))
    send(3)
    start_mean(0, pres)
    near = local_rows(pres)
    theta_next = theta_finish(theta, net, receive(7))
    force = couple * (theta_next - theta) / NS
    t_out[0] = theta_next
    pres, prev = advance(pres, prev, near, halo_rows(receive(3)), degree, force)
    store_rows(4, export(pres))
    send(4)
    near = local_rows(pres)
    turn_mean(0)
    pres, prev = advance(pres, prev, near, halo_rows(receive(4)), degree, force)
    store_rows(5, export(pres))
    send(5)
    near = local_rows(pres)
    first_mean = spread_row(end_mean(0))
    pres, prev = advance(pres, prev, near, halo_rows(receive(5)), degree, force)
    current = less_mean(pres, first_mean)
    cur_buf[...] = current

    band = LV // n_mem

    def scatter_copy(k):
        peer = (m + k) % n_mem
        return pltpu.make_async_remote_copy(
            src_ref=cur_buf.at[pl.ds(pl.multiple_of(peer * band, band), band), :],
            dst_ref=rs_box.at[m],
            send_sem=x_send.at[0, k],
            recv_sem=x_recv.at[0, k],
            device_id=members[k - 1],
            device_id_type=MESH,
        )

    def gather_copy(k):
        return pltpu.make_async_remote_copy(
            src_ref=slab,
            dst_ref=ens.at[m],
            send_sem=x_send.at[1, k],
            recv_sem=x_recv.at[1, k],
            device_id=members[k - 1],
            device_id_type=MESH,
        )

    def mean_copy(k):
        return pltpu.make_async_remote_copy(
            src_ref=row_m,
            dst_ref=box_m.at[m],
            send_sem=x_send.at[2, k],
            recv_sem=x_recv.at[2, k],
            device_id=members[k - 1],
            device_id_type=MESH,
        )

    for k in range(1, n_mem):
        scatter_copy(k).start()
    start_mean(1, current)
    rs_box[m] = cur_buf[pl.ds(pl.multiple_of(m * band, band), band), :]
    for k in range(1, n_mem):
        scatter_copy(k).wait_recv()
    total = jnp.sum(rs_box[...], axis=0)
    slab[...] = total
    ens[m] = total
    for k in range(1, n_mem):
        gather_copy(k).start()
    turn_mean(1)
    row = end_mean(1)
    row_m[...] = row
    box_m[m] = row
    for k in range(1, n_mem):
        mean_copy(k).start()
    p_out[0] = less_mean(current, spread_row(row))
    for k in range(1, n_mem):
        gather_copy(k).wait_recv()
    for k in range(1, n_mem):
        mean_copy(k).wait_recv()
    all_means = spread_row(jnp.sum(box_m[...], axis=0))
    summed = jnp.concatenate([ens[i] for i in range(n_mem)], axis=0)
    e_out[...] = less_mean(summed, all_means) / n_mem

    for slot in range(8):
        for b in range(NBK):
            halo_copy(slot, b).wait_send()
    for which in range(2):
        for k in range(1, LINE):
            line_copy(which, k).wait_send()
        for k in range(1, n_line):
            across_copy(which, k).wait_send()
    for k in range(1, n_mem):
        scatter_copy(k).wait_send()
        gather_copy(k).wait_send()
        mean_copy(k).wait_send()


def per_device(
    acoustic_perturbation,
    prior_acoustic_state,
    thermal_anomaly,
    model_parameters,
    crossing_velocity,
    face_extent,
    face_metric_factor,
    reciprocal_polygon_surface,
    owned_totals,
    export_lists,
    face_neighbour_pair,
    polygon_side_lookup,
):
    n_mem = lax.axis_size("member")
    n_line = lax.axis_size("dom") // LINE
    band = LV // n_mem
    smalls = jnp.stack([face_extent, face_metric_factor])
    vmem = pl.BlockSpec(memory_space=pltpu.VMEM)
    smem = pl.BlockSpec(memory_space=pltpu.SMEM)
    dma = pltpu.SemaphoreType.DMA
    return pl.pallas_call(
        kernel,
        out_shape=(
            jax.ShapeDtypeStruct((1, LV, CC), F32),
            jax.ShapeDtypeStruct((1, LV, CC), F32),
            jax.ShapeDtypeStruct((LV, CC), F32),
        ),
        in_specs=[smem, smem] + [vmem] * 8,
        out_specs=(vmem, vmem, vmem),
        scratch_shapes=[
            pltpu.VMEM((3, EXT, CC), BF16),
            pltpu.VMEM((2, EXT, CC), BF16),
            pltpu.VMEM((CC, HALO), BF16),
            pltpu.VMEM((3, LV, CC), F32),
            pltpu.VMEM((3, 8, CC), F32),
            pltpu.VMEM((8, NBK, LV, HB), F32),
            pltpu.VMEM((8, NBK, LV, HB), F32),
            pltpu.VMEM((2, 1, HB), F32),
            pltpu.VMEM((2, 1, HB), F32),
            pltpu.VMEM((1, HB), F32),
            pltpu.VMEM((2, LINE, 1, HB), F32),
            pltpu.VMEM((2, n_line, 1, HB), F32),
            pltpu.VMEM((n_mem, 1, HB), F32),
            pltpu.VMEM((LV, CC), F32),
            pltpu.VMEM((n_mem, band, CC), F32),
            pltpu.VMEM((band, CC), F32),
            pltpu.VMEM((n_mem, band, CC), F32),
            dma((8, NBK)),
            dma((8, NBK)),
            dma((2, LINE + n_line)),
            dma((2, LINE + n_line)),
            dma((3, n_mem)),
            dma((3, n_mem)),
        ],
        compiler_params=pltpu.CompilerParams(collective_id=0, has_side_effects=True),
    )(
        model_parameters,
        owned_totals,
        acoustic_perturbation,
        prior_acoustic_state,
        thermal_anomaly,
        crossing_velocity,
        smalls,
        reciprocal_polygon_surface[None, :],
        export_lists,
        face_neighbour_pair,
    )


def solution(mesh):
    in_specs = (
        P("member", None, "dom"),
        P("member", None, "dom"),
        P("member", None, "dom"),
        P("member", None),
        P(None, "dom"),
        P("dom"),
        P("dom"),
        P("dom"),
        P("dom"),
        P("dom", None, None),
        P(None, "dom"),
        P(None, "dom"),
    )
    out_specs = (P("member", None, "dom"), P("member", None, "dom"), P(None, "dom"))
    return jax.shard_map(
        per_device, mesh=mesh, in_specs=in_specs, out_specs=out_specs, check_vma=False
    )
```

time: 616 us -> 73.3 us (0.12); the launches traced: 604 us -> 72.5 us
  matrix products: 185 us -> 0 us
  local copies, waits for them, and re-layouts: 177 us -> 4.5 us
  starting transfers between devices: 111 us -> 0 us
  other arithmetic: 92.7 us -> 1.34 us
  Pallas kernels: 0 us -> 65.4 us
  blocking collectives: 23.8 us -> 0 us
  waiting for transfers between devices: 8.2 us -> 0 us
    dot_general x132 -> x0, matrix products: 179 us -> none  [exact_dot(): jnp.dot(left_side, right_side, precision=lax.Precision.HIGHEST, preferred...]
    ppermute x36 -> x0, starting transfers between devices: 92.1 us -> none  [passed_along(): return lax.ppermute(block, axis, route)]
    pallas_call x0 -> x1, Pallas kernels: none -> 65.4 us  [per_device(): pl.pallas_call(kernel, out_shape=(jax.ShapeDtypeStruct((1, LV, CC), F32),...]
    reshape x24 -> x0, local copies, waits for them, and re-layouts: 54.7 us -> none  [the longest x10 31.1 us: starts_of(): jnp.broadcast_to(fields[:, :, None], (levels, cell_count, 3))]
    reduce_sum x13 -> x0, other arithmetic: 52.5 us -> none  [the longest x8 50.5 us: divergence(): outgoing = jnp.sum(fluxes.reshape(levels, cell_count, 3), axis=2)]
    unnamed x144 -> x10, local copies, waits for them, and re-layouts: 38.6 us -> 4.5 us
    dynamic_slice x144 -> x0, local copies, waits for them, and re-layouts: 28.9 us -> none  [the longest x16 16.5 us: divergence(): lax.scan(add_block, jnp.zeros((levels, cell_count), jnp.float32), (index_...]
    all_to_all x1 -> x0, blocking collectives: 23.8 us -> none  [from_everyone(): return lax.all_to_all(copies, axis, split_axis=0, concat_axis=0, tiled=True)]
  transfers between devices with their start and end apart: 38 -> 0, of which waited for: 4 -> 0; matrix products, arithmetic and copies ran while one was open for 12% -> 0% of each run, Pallas kernels for 0% -> 0%
where the time goes in v1:
time: 73.3 us; the launch traced here: 72.5 us
  Pallas kernels  65.4 us (89%)
  local copies, waits for them, and re-layouts  4.5 us (6%)
  other arithmetic  1.34 us (2%)
  between operations  1.32 us (2%)
    pallas_call x1, Pallas kernels, per_device(): pl.pallas_call(kernel, out_shape=(jax.ShapeDtypeStruct((1, LV, CC), F32),...  65.4 us
    unnamed x10, local copies, waits for them, and re-layouts  4.5 us

profile of v1, /device:TPU:1, one launch (start us, length us, event | category | flops | bytes accessed | tf_op | source)
XLA Modules:
  0.0 72.5 jit_solution(3352842547424263221)
XLA Ops:
  0.6 0.0 copy-start.2
  1.3 1.3 %copy.14.exp_in = s32[1,6,128]{2,1,0:T(8,128)} copy(s32[1,6,128]{2,0,1:T(1,128)} %param.21) | data formatting | bytes 6144 | tf_op args[9]
  2.6 0.0 copy-done.2
  2.6 1.3 %pad_maximum_fusion.small_in = f32[2,3072]{1,0:T(2,128)} fusion(f32[1,3072]{1,0:T(1,128)S(1)} %bitcast.3, f32[1,3072]{1,0:T(1,128)} %bitcast.4), kind=kLoop, calls=%fused_computation | loop fusion | flops 6144 | bytes 49152 | tf_op jit(solution)/shard_map/stack | solution.py:423
  3.9 65.4 %shard_map.130 = (f32[1,32,1024]{2,1,0:T(8,128)}, f32[1,32,1024]{2,1,0:T(8,128)}, f32[32,1024]{1,0:T(8,128)}) custom-call(f32[1,4]{1,0:T(1,128)} %par.1, s32[1]{0:T(128)S(6)} %copy.18.tot, f32[1,32,1024]{2,1,0:T(8,128)} %p_in.1, f32[1,32,1024]{2,1,0:T(8,128)} %q_in.1, f32[1,32,1024]{2,1,0:T(8,128)} %t_in.1, f32[32,3072]{1,0:T(8,128)} %v_in.1, ...), custom_call_target="tpu_custom_call" | custom-call | tf_op jit(solution)/shard_map/pallas_call | solution.py:427
  69.3 0.0 copy-start.1
  69.3 1.6 %copy.19 = f32[1,32,1024]{2,1,0:T(8,128)} copy(f32[1,32,1024]{2,1,0:T(8,128)} %get-tuple-element.6) | data formatting | bytes 262144
  70.9 0.0 copy-done.1
  70.9 0.0 copy-start
  70.9 0.7 copy.20
  71.6 0.3 copy-done
  71.9 0.7 copy.21
Async XLA Ops:
  0.6 1.9 %copy-start.2 = (f32[3072]{0:T(1024)S(1)}, f32[3072]{0:T(1024)}, u32[]{:S(2)}) copy-start(f32[3072]{0:T(1024)} %param.18) | copy-start | bytes 36868
  69.3 1.6 %copy-start.1 = (f32[1,32,1024]{2,1,0:T(8,128)S(1)}, f32[1,32,1024]{2,1,0:T(8,128)}, u32[]{:S(2)}) copy-start(f32[1,32,1024]{2,1,0:T(8,128)} %get-tuple-element.7) | copy-start | bytes 393220
  70.9 1.0 %copy-start = (f32[32,1024]{1,0:T(8,128)S(1)}, f32[32,1024]{1,0:T(8,128)}, u32[]{:S(2)}) copy-start(f32[32,1024]{1,0:T(8,128)} %get-tuple-element.8) | copy-start | bytes 393220

commit v2 on v1

v2 whole, which is shorter than its diff:
```python
import jax
import jax.numpy as jnp
from jax import lax
from jax.experimental import pallas as pl
from jax.experimental.pallas import tpu as pltpu
from jax.sharding import PartitionSpec as P

MESH = pl.DeviceIdType.MESH
F32 = jnp.float32
BF16 = jnp.bfloat16
F8 = jnp.float8_e4m3fn

LV = 32
CC = 1024
NBK = 6
HB = 128
HALO = NBK * HB
EXT = CC + HALO
LINE = 16
DT = 0.25
NS = 3
OFFSETS = [(b // 2 + 1) * (1 - 2 * (b % 2)) for b in range(NBK)]
SEND_ORDER = (4, 5, 2, 3, 0, 1)


def split2(x):
    hi = x.astype(BF16)
    lo = (x - hi.astype(F32)).astype(BF16)
    return hi, lo


def rows2(*fields):
    return jnp.concatenate([part for x in fields for part in split2(x)], axis=0)


def split3(x):
    a = x.astype(BF16)
    r = x - a.astype(F32)
    b = r.astype(BF16)
    c = (r - b.astype(F32)).astype(BF16)
    return a, b, c


def mm(a, b):
    return jnp.dot(a, b, preferred_element_type=F32)


def mm_t(a, b):
    return lax.dot_general(a, b, (((1,), (1,)), ((), ())), preferred_element_type=F32)


def fold(o, i=0):
    return o[2 * i * LV : (2 * i + 1) * LV] + o[(2 * i + 1) * LV : (2 * i + 2) * LV]


def kernel(
    par, tot, p_hbm, q_hbm, t_hbm, v_hbm, len_in, met_in, inv_in, exp_in, end_in,
    p_out, t_out, e_out,
    p_in, q_in, t_in, v_in, sel, esel, vd, sd, snd, rcv, row_a, row_b, box_a, box_b, box_x,
    cur_buf, rs_box, slab, ens, in_sem, s_send, s_recv, a_send, a_recv, b_send, b_recv, x_send, x_recv,
):
    n_mem = lax.axis_size("member")
    n_dom = lax.axis_size("dom")
    n_line = n_dom // LINE
    m = lax.axis_index("member")
    d = lax.axis_index("dom")
    line, pos = d // LINE, d % LINE

    loads = [
        pltpu.make_async_copy(src, dst, in_sem.at[i])
        for i, (src, dst) in enumerate(((t_hbm.at[0], t_in), (p_hbm.at[0], p_in), (v_hbm, v_in), (q_hbm.at[0], q_in)))
    ]
    for load in loads:
        load.start()

    neighbours = [(m, (d + off + n_dom) % n_dom) for off in OFFSETS]
    in_line = [(m, line * LINE + (pos + k) % LINE) for k in range(1, LINE)]
    shifts = [(i, k) for i in range(n_mem) for k in range(n_line) if i or k]
    across = [((m + i) % n_mem, (d + k * LINE) % n_dom) for i, k in shifts]
    members = [((m + k) % n_mem, d) for k in range(1, n_mem)]

    barrier = pltpu.get_barrier_semaphore()
    peers = neighbours + in_line + across
    for peer in peers:
        pl.semaphore_signal(barrier, inc=1, device_id=peer, device_id_type=MESH)

    speed = par[0, 0]
    kappa = 0.5 * par[0, 1]
    mixing = 0.6 * par[0, 2]
    couple = par[0, 3]
    owned = lax.broadcasted_iota(jnp.int32, (1, CC), 1) < tot[0]
    inv = inv_in[...]
    iota32 = lax.broadcasted_iota(jnp.int32, (32, HB), 0).astype(F32).astype(BF16)
    one = jnp.full((32, HB), 1.0, BF16)
    zero = jnp.full((32, HB), 0.0, BF16)

    def packed_row(row):
        return jnp.broadcast_to(jnp.clip(row, -1.0, 256.0), (32, HB)).astype(BF16)

    def hot(r, want):
        return jnp.where(iota32 + jnp.asarray(32.0 * r, BF16) == want, one, zero).astype(F8)

    def build_exports(t, carry):
        base = pl.multiple_of(t * 256, 256)
        for b in range(NBK):
            want = packed_row(exp_in[b].astype(F32) - (t * 256).astype(F32))
            for r in range(8):
                esel[pl.ds(base + 32 * r, 32), b * HB : (b + 1) * HB] = hot(r, want)
        return carry

    lax.fori_loop(0, CC // 256, build_exports, 0)

    def store_rows(slot, values):
        for b in range(NBK):
            snd[slot, b] = values[:, b * HB : (b + 1) * HB]

    def halo_copy(slot, b):
        return pltpu.make_async_remote_copy(
            src_ref=snd.at[slot, b],
            dst_ref=rcv.at[slot, b],
            send_sem=s_send.at[slot, b],
            recv_sem=s_recv.at[slot, b],
            device_id=neighbours[b],
            device_id_type=MESH,
        )

    def send(slot):
        for b in SEND_ORDER:
            halo_copy(slot, b).start()

    def receive(slot):
        for b in range(NBK):
            halo_copy(slot, b).wait_recv()
        return jnp.concatenate([rcv[slot, b] for b in range(NBK)], axis=1)

    loads[0].wait()
    loads[1].wait()
    theta = t_in[...]
    pres = p_in[...]
    both = mm(rows2(theta, pres), esel[...])
    store_rows(6, fold(both, 0))
    store_rows(0, fold(both, 1))

    er = lax.broadcasted_iota(jnp.int32, (3 * HB, 3 * HB), 0)
    ec = lax.broadcasted_iota(jnp.int32, (3 * HB, 3 * HB), 1)
    order = jnp.where(er == 3 * (ec % HB) + ec // HB, 1.0, 0.0).astype(F32).astype(BF16)
    ends = end_in[1:2, :]
    end_hi = (ends // 256).astype(F32)
    end_lo = (ends % 256).astype(F32)
    smalls = jnp.concatenate([end_hi, end_lo, len_in[...], met_in[...], jnp.zeros((4, 3 * CC), F32)], axis=0)
    smalls = jnp.concatenate(
        [part.astype(F32) for part in split3(smalls)] + [jnp.zeros((8, 3 * CC), F32)], axis=0
    ).astype(BF16)
    loads[2].wait()
    stacked = rows2(v_in[...])
    for g in range(CC // HB):
        cols = slice(g * 3 * HB, (g + 1) * 3 * HB)
        o = mm(jnp.concatenate([stacked[:, cols], smalls[:, cols]], axis=0), order)
        vel = fold(o)
        small = o[64:72] + o[72:80] + o[80:88]
        for j in range(3):
            vd[j, :, g * HB : (g + 1) * HB] = vel[:, j * HB : (j + 1) * HB]
            sd[j, :, g * HB : (g + 1) * HB] = small[:, j * HB : (j + 1) * HB]

    def build(t, carry):
        base = pl.multiple_of(t * 256, 256)
        tf = t.astype(F32)
        for g in range(CC // HB):
            lanes = slice(g * HB, (g + 1) * HB)
            for j in range(3):
                want = packed_row((sd[j, 0:1, lanes] - tf) * 256.0 + sd[j, 1:2, lanes])
                for r in range(8):
                    sel[j, pl.ds(base + 32 * r, 32), lanes] = hot(r, want)
        return carry

    lax.fori_loop(0, CC // 256, build, 0)
    pl.semaphore_wait(barrier, len(peers))
    send(6)
    send(0)
    lax.fori_loop(CC // 256, EXT // 256, build, 0)

    def coefficients(j):
        v = vd[j]
        length = sd[j, 2:3, :]
        return length * (jnp.maximum(v, 0.0) + kappa), length * (jnp.minimum(v, 0.0) - kappa)

    def weight(j):
        return sd[j, 3:4, :]

    def near_both(p, th):
        lhs = rows2(p, th)
        net_p, net_t = jnp.zeros((LV, CC), F32), jnp.zeros((LV, CC), F32)
        for j in range(3):
            ends_of = mm(lhs, sel[j, :CC, :])
            start, end = coefficients(j)
            grad = weight(j) * (fold(ends_of, 0) - p)
            flux = start * th + end * fold(ends_of, 1)
            incoming = mm_t(rows2(grad, flux), sel[j, :CC, :])
            net_p = net_p + grad - fold(incoming, 0)
            net_t = net_t + flux - fold(incoming, 1)
        return net_p, net_t

    def near_pressure(p):
        lhs = rows2(p)
        net = jnp.zeros((LV, CC), F32)
        for j in range(3):
            grad = weight(j) * (fold(mm(lhs, sel[j, :CC, :])) - p)
            net = net + grad - fold(mm_t(rows2(grad), sel[j, :CC, :]))
        return net

    def far_pressure(halo, net):
        lhs = rows2(halo)
        for j in range(3):
            net = net + weight(j) * fold(mm(lhs, sel[j, CC:, :]))
        return net

    def far_theta(halo, net):
        lhs = rows2(halo)
        for j in range(3):
            net = net + coefficients(j)[1] * fold(mm(lhs, sel[j, CC:, :]))
        return net

    def advance_theta(th, net):
        up = jnp.concatenate([th[1:], th[LV - 1 :]], axis=0) - th
        down = th - jnp.concatenate([th[:1], th[: LV - 1]], axis=0)
        return jnp.where(owned, th + DT * (mixing * (up - down) - inv * net), th)

    scale = speed * inv

    def advance(p, q, net, force):
        return jnp.where(owned, 2.0 * p - q + scale * net + force, p), p

    def export(p):
        return fold(mm(rows2(p), esel[...]))

    area = jnp.where(owned, 1.0 / inv, 0.0)

    def partial_row(p):
        total = jnp.zeros((LV, HB), F32)
        spread = jnp.zeros((1, HB), F32)
        for g in range(CC // HB):
            lanes = slice(g * HB, (g + 1) * HB)
            total = total + p[:, lanes] * area[:, lanes]
            spread = spread + area[:, lanes]
        padded = jnp.concatenate([total, spread, jnp.zeros((HB - LV - 1, HB), F32)], axis=0)
        return jnp.sum(padded.T, axis=0, keepdims=True)

    def spread_row(row):
        return jnp.broadcast_to(row, (HB, HB)).T[:LV]

    def line_copy(which, k):
        return pltpu.make_async_remote_copy(
            src_ref=row_a.at[which],
            dst_ref=box_a.at[which, pos],
            send_sem=a_send.at[which, k],
            recv_sem=a_recv.at[which, k],
            device_id=in_line[k - 1],
            device_id_type=MESH,
        )

    def across_copy(k):
        return pltpu.make_async_remote_copy(
            src_ref=row_b.at[0],
            dst_ref=box_b.at[line],
            send_sem=b_send.at[0, k],
            recv_sem=b_recv.at[0, k],
            device_id=(m, (d + k * LINE) % n_dom),
            device_id_type=MESH,
        )

    def wide_copy(n):
        return pltpu.make_async_remote_copy(
            src_ref=row_b.at[1],
            dst_ref=box_x.at[m, line],
            send_sem=b_send.at[1, n],
            recv_sem=b_recv.at[1, n],
            device_id=across[n],
            device_id_type=MESH,
        )

    def start_mean(which, p):
        row = partial_row(p)
        row_a[which] = row
        box_a[which, pos] = row
        for k in range(1, LINE):
            line_copy(which, k).start()

    def line_sum(which):
        for k in range(1, LINE):
            line_copy(which, k).wait_recv()
        row = jnp.sum(box_a[which], axis=0)
        row_b[which] = row
        return row

    def level_mean(rows):
        row = jnp.sum(rows, axis=0)
        return row / row[:, LV : LV + 1]

    def less_mean(p, mean):
        wide = jnp.concatenate([spread_row(mean)] * (CC // HB), axis=1)
        return p - jnp.where(owned, wide, 0.0)

    net, net_theta = near_both(pres, theta)
    theta_next = advance_theta(theta, far_theta(receive(6), net_theta))
    force = couple * (theta_next - theta) / NS
    theta = theta_next
    net = far_pressure(receive(0), net)
    loads[3].wait()
    pres, prev = advance(pres, q_in[...], net, force)
    store_rows(1, export(pres))
    send(1)
    store_rows(7, export(theta))
    send(7)
    net = near_pressure(pres)
    pres, prev = advance(pres, prev, far_pressure(receive(1), net), force)
    store_rows(2, export(pres))
    send(2)
    net, net_theta = near_both(pres, theta)
    pres, prev = advance(pres, prev, far_pressure(receive(2), net), force)
    store_rows(3, export(pres))
    send(3)
    start_mean(0, pres)
    net = near_pressure(pres)
    theta_next = advance_theta(theta, far_theta(receive(7), net_theta))
    force = couple * (theta_next - theta) / NS
    t_out[...] = theta_next
    pres, prev = advance(pres, prev, far_pressure(receive(3), net), force)
    store_rows(4, export(pres))
    send(4)
    net = near_pressure(pres)
    row = line_sum(0)
    box_b[line] = row
    for k in range(1, n_line):
        across_copy(k).start()
    pres, prev = advance(pres, prev, far_pressure(receive(4), net), force)
    store_rows(5, export(pres))
    send(5)
    net = near_pressure(pres)
    for k in range(1, n_line):
        across_copy(k).wait_recv()
    first_mean = level_mean(box_b[...])
    pres, prev = advance(pres, prev, far_pressure(receive(5), net), force)
    current = less_mean(pres, first_mean)
    cur_buf[...] = current

    band = LV // n_mem

    def scatter_copy(k):
        peer = (m + k) % n_mem
        return pltpu.make_async_remote_copy(
            src_ref=cur_buf.at[pl.ds(pl.multiple_of(peer * band, band), band), :],
            dst_ref=rs_box.at[m],
            send_sem=x_send.at[0, k],
            recv_sem=x_recv.at[0, k],
            device_id=members[k - 1],
            device_id_type=MESH,
        )

    def gather_copy(k):
        return pltpu.make_async_remote_copy(
            src_ref=slab,
            dst_ref=ens.at[m],
            send_sem=x_send.at[1, k],
            recv_sem=x_recv.at[1, k],
            device_id=members[k - 1],
            device_id_type=MESH,
        )

    for k in range(1, n_mem):
        scatter_copy(k).start()
    start_mean(1, current)
    rs_box[m] = cur_buf[pl.ds(pl.multiple_of(m * band, band), band), :]
    for k in range(1, n_mem):
        scatter_copy(k).wait_recv()
    total = jnp.sum(rs_box[...], axis=0)
    slab[...] = total
    ens[m] = total
    for k in range(1, n_mem):
        gather_copy(k).start()
    row = line_sum(1)
    box_x[m, line] = row
    for n in range(len(shifts)):
        wide_copy(n).start()
    for k in range(1, n_mem):
        gather_copy(k).wait_recv()
    for n in range(len(shifts)):
        wide_copy(n).wait_recv()
    p_out[...] = less_mean(current, level_mean(box_x[m]))
    all_means = level_mean(box_x[0])
    for i in range(1, n_mem):
        all_means = all_means + level_mean(box_x[i])
    summed = jnp.concatenate([ens[i] for i in range(n_mem)], axis=0)
    e_out[...] = less_mean(summed, all_means) / n_mem

    for slot in range(8):
        for b in range(NBK):
            halo_copy(slot, b).wait_send()
    for which in range(2):
        for k in range(1, LINE):
            line_copy(which, k).wait_send()
    for k in range(1, n_line):
        across_copy(k).wait_send()
    for n in range(len(shifts)):
        wide_copy(n).wait_send()
    for k in range(1, n_mem):
        scatter_copy(k).wait_send()
        gather_copy(k).wait_send()


def hand_over(p, t, e, p_out, t_out, e_out, sem):
    moves = [
        pltpu.make_async_copy(src, dst, sem.at[i])
        for i, (src, dst) in enumerate(((p, p_out.at[0]), (t, t_out.at[0]), (e, e_out)))
    ]
    for move in moves:
        move.start()
    for move in moves:
        move.wait()


def per_device(
    acoustic_perturbation,
    prior_acoustic_state,
    thermal_anomaly,
    model_parameters,
    crossing_velocity,
    face_extent,
    face_metric_factor,
    reciprocal_polygon_surface,
    owned_totals,
    export_lists,
    face_neighbour_pair,
    polygon_side_lookup,
):
    n_mem = lax.axis_size("member")
    n_line = lax.axis_size("dom") // LINE
    n_wide = n_mem * n_line - 1
    band = LV // n_mem
    vmem = pl.BlockSpec(memory_space=pltpu.VMEM)
    smem = pl.BlockSpec(memory_space=pltpu.SMEM)
    anyw = pl.BlockSpec(memory_space=pl.ANY)
    dma = pltpu.SemaphoreType.DMA
    held = pl.pallas_call(
        kernel,
        out_shape=tuple(pltpu.VMEM((LV, CC), F32) for _ in range(3)),
        in_specs=[smem, smem] + [anyw] * 4 + [vmem] * 5,
        out_specs=(vmem, vmem, vmem),
        scratch_shapes=[
            pltpu.VMEM((LV, CC), F32),
            pltpu.VMEM((LV, CC), F32),
            pltpu.VMEM((LV, CC), F32),
            pltpu.VMEM((LV, 3 * CC), F32),
            pltpu.VMEM((3, EXT, CC), F8),
            pltpu.VMEM((CC, HALO), F8),
            pltpu.VMEM((3, LV, CC), F32),
            pltpu.VMEM((3, 8, CC), F32),
            pltpu.VMEM((8, NBK, LV, HB), F32),
            pltpu.VMEM((8, NBK, LV, HB), F32),
            pltpu.VMEM((2, 1, HB), F32),
            pltpu.VMEM((2, 1, HB), F32),
            pltpu.VMEM((2, LINE, 1, HB), F32),
            pltpu.VMEM((n_line, 1, HB), F32),
            pltpu.VMEM((n_mem, n_line, 1, HB), F32),
            pltpu.VMEM((LV, CC), F32),
            pltpu.VMEM((n_mem, band, CC), F32),
            pltpu.VMEM((band, CC), F32),
            pltpu.VMEM((n_mem, band, CC), F32),
            dma((4,)),
            dma((8, NBK)),
            dma((8, NBK)),
            dma((2, LINE)),
            dma((2, LINE)),
            dma((2, n_wide)),
            dma((2, n_wide)),
            dma((2, n_mem)),
            dma((2, n_mem)),
        ],
        compiler_params=pltpu.CompilerParams(collective_id=0, has_side_effects=True),
    )(
        model_parameters,
        owned_totals,
        acoustic_perturbation,
        prior_acoustic_state,
        thermal_anomaly,
        crossing_velocity,
        face_extent[None, :],
        face_metric_factor[None, :],
        reciprocal_polygon_surface[None, :],
        export_lists.reshape(NBK, 1, HB),
        face_neighbour_pair,
    )
    return pl.pallas_call(
        hand_over,
        out_shape=(
            jax.ShapeDtypeStruct((1, LV, CC), F32),
            jax.ShapeDtypeStruct((1, LV, CC), F32),
            jax.ShapeDtypeStruct((LV, CC), F32),
        ),
        in_specs=[vmem] * 3,
        out_specs=(anyw, anyw, anyw),
        scratch_shapes=[dma((3,))],
    )(*[pltpu.with_memory_space_constraint(x, pltpu.VMEM) for x in held])


def solution(mesh):
    in_specs = (
        P("member", None, "dom"),
        P("member", None, "dom"),
        P("member", None, "dom"),
        P("member", None),
        P(None, "dom"),
        P("dom"),
        P("dom"),
        P("dom"),
        P("dom"),
        P("dom", None, None),
        P(None, "dom"),
        P(None, "dom"),
    )
    out_specs = (P("member", None, "dom"), P("member", None, "dom"), P(None, "dom"))
    return jax.shard_map(
        per_device, mesh=mesh, in_specs=in_specs, out_specs=out_specs, check_vma=False
    )
```

time: 73.3 us -> 56.3 us (0.77)
  Pallas kernels: 65.4 us -> 54.8 us
  local copies, waits for them, and re-layouts: 4.5 us -> 0 us
  other arithmetic: 1.34 us -> 0 us
    pallas_call x1 -> x2, Pallas kernels: 65.4 us -> 54.8 us  [the longest x1 54.1 us: per_device(): pl.pallas_call(kernel, out_shape=tuple((pltpu.VMEM((LV, CC), F32) for _ i...]
    unnamed x10 -> x0, local copies, waits for them, and re-layouts: 4.5 us -> none
    another operation x1 -> x0, other arithmetic: 1.34 us -> none  [per_device(): smalls = jnp.stack([face_extent, face_metric_factor])]
where the time goes in v2:
time: 56.3 us; the launch traced here: 56.1 us
  Pallas kernels  54.8 us (97%)
  between operations  1.29 us (2%)
    pallas_call x1, Pallas kernels, per_device(): pl.pallas_call(kernel, out_shape=tuple((pltpu.VMEM((LV, CC), F32) for _ i...  54.1 us

profile of v2, /device:TPU:1, one launch (start us, length us, event | category | flops | bytes accessed | tf_op | source)
XLA Modules:
  0.0 56.1 jit_solution(303746502717049936)
XLA Ops:
  1.3 54.1 %shard_map.130 = (f32[32,1024]{1,0:T(8,128)S(1)}, f32[32,1024]{1,0:T(8,128)S(1)}, f32[32,1024]{1,0:T(8,128)S(1)}) custom-call(f32[1,4]{1,0:T(1,128)} %par.1, s32[1]{0:T(128)S(6)} %copy.14.tot, f32[1,32,1024]{2,1,0:T(8,128)} %p_hbm.1, f32[1,32,1024]{2,1,0:T(8,128)} %q_hbm.1, f32[1,32,1024]{2,1,0:T(8,128)} %t_hbm.1, f32[32,3072]{1,0:T(8,128)} %v_hbm.1, ...), custom_call_target="tpu_custom_call" | custom-call | tf_op jit(solution)/shard_map/pallas_call | solution.py:443
  55.3 0.8 %shard_map.131 = (f32[1,32,1024]{2,1,0:T(8,128)}, f32[1,32,1024]{2,1,0:T(8,128)}, f32[32,1024]{1,0:T(8,128)}) custom-call(f32[32,1024]{1,0:T(8,128)S(1)} %get-tuple-element.6.p, f32[32,1024]{1,0:T(8,128)S(1)} %get-tuple-element.7.t, f32[32,1024]{1,0:T(8,128)S(1)} %get-tuple-element.8.e), custom_call_target="tpu_custom_call" | custom-call | tf_op jit(solution)/shard_map/pallas_call | solution.py:492

commit v3 on v2

v3 whole, which is shorter than its diff:
```python
import jax
import jax.numpy as jnp
from jax import lax
from jax.experimental import pallas as pl
from jax.experimental.pallas import tpu as pltpu
from jax.sharding import PartitionSpec as P

MESH = pl.DeviceIdType.MESH
F32 = jnp.float32
BF16 = jnp.bfloat16
F8 = jnp.float8_e4m3fn

LV = 32
CC = 1024
NBK = 6
HB = 128
HALO = NBK * HB
EXT = CC + HALO
LINE = 16
DT = 0.25
NS = 3
OFFSETS = [(b // 2 + 1) * (1 - 2 * (b % 2)) for b in range(NBK)]
SEND_ORDER = (4, 5, 2, 3, 0, 1)
NEAR = 4


def split2(x):
    hi = x.astype(BF16)
    lo = (x - hi.astype(F32)).astype(BF16)
    return hi, lo


def rows2(*fields):
    return jnp.concatenate([part for x in fields for part in split2(x)], axis=0)


def split3(x):
    a = x.astype(BF16)
    r = x - a.astype(F32)
    b = r.astype(BF16)
    c = (r - b.astype(F32)).astype(BF16)
    return a, b, c


def mm(a, b):
    return jnp.dot(a, b, preferred_element_type=F32)


def mm_t(a, b):
    return lax.dot_general(a, b, (((1,), (1,)), ((), ())), preferred_element_type=F32)


def fold(o, i=0):
    return o[2 * i * LV : (2 * i + 1) * LV] + o[(2 * i + 1) * LV : (2 * i + 2) * LV]


def kernel(
    par_hbm, p_hbm, q_hbm, t_hbm, v_hbm, len_hbm, met_hbm, inv_hbm, exp_hbm, end_hbm,
    p_out, t_out, e_out,
    par, p_in, q_in, t_in, v_in, len_in, met_in, inv_in, exp_in, end_in,
    sel, esel, vd, sd, snd, rcv, reach, reach_in, row_a, row_b, box_a, box_x, cur_buf, rs_box, slab, ens,
    in_sem, s_send, s_recv, h_sem, a_send, a_recv, b_send, b_recv, x_send, x_recv,
):
    n_mem = lax.axis_size("member")
    n_dom = lax.axis_size("dom")
    n_line = n_dom // LINE
    m = lax.axis_index("member")
    d = lax.axis_index("dom")
    line, pos = d // LINE, d % LINE

    neighbours = [(m, (d + off + n_dom) % n_dom) for off in OFFSETS]
    in_line = [(m, line * LINE + (pos + k) % LINE) for k in range(1, LINE)]
    shifts = [(i, k) for i in range(n_mem) for k in range(n_line) if i or k]
    across = [((m + i) % n_mem, (d + k * LINE) % n_dom) for i, k in shifts]

    barrier = pltpu.get_barrier_semaphore()
    peers = neighbours + in_line + across
    for peer in peers:
        pl.semaphore_signal(barrier, inc=1, device_id=peer, device_id_type=MESH)

    sources = (exp_hbm, t_hbm.at[0], p_hbm.at[0], end_hbm, len_hbm, met_hbm, v_hbm, inv_hbm, par_hbm, q_hbm.at[0])
    targets = (exp_in, t_in, p_in, end_in, len_in, met_in, v_in, inv_in, par, q_in)
    groups = (0, 1, 1, 2, 2, 2, 3, 3, 3, 3)
    loads = [
        pltpu.make_async_copy(src, dst, in_sem.at[i]) for i, (src, dst) in enumerate(zip(sources, targets))
    ]
    for load in loads:
        load.start()

    def loaded(group):
        for load, its in zip(loads, groups):
            if its == group:
                load.wait()

    iota32 = lax.broadcasted_iota(jnp.int32, (32, HB), 0).astype(F32).astype(BF16)
    one = jnp.full((32, HB), 1.0, BF16)
    zero = jnp.full((32, HB), 0.0, BF16)

    def packed_row(row):
        return jnp.broadcast_to(jnp.clip(row, -1.0, 256.0), (32, HB)).astype(BF16)

    def hot(r, want):
        return jnp.where(iota32 + jnp.asarray(32.0 * r, BF16) == want, one, zero).astype(F8)

    loaded(0)

    def build_exports(t, carry):
        base = pl.multiple_of(t * 256, 256)
        for b in range(NBK):
            want = packed_row(exp_in[b].astype(F32) - (t * 256).astype(F32))
            for r in range(8):
                esel[pl.ds(base + 32 * r, 32), b * HB : (b + 1) * HB] = hot(r, want)
        return carry

    lax.fori_loop(0, CC // 256, build_exports, 0)

    def halo_copy(slot, b):
        return pltpu.make_async_remote_copy(
            src_ref=snd.at[slot, b],
            dst_ref=rcv.at[slot, b],
            send_sem=s_send,
            recv_sem=s_recv.at[slot, b // NEAR],
            device_id=neighbours[b],
            device_id_type=MESH,
        )

    def export_and_send(*slots_and_fields):
        slots, fields = slots_and_fields[::2], slots_and_fields[1::2]
        lhs = rows2(*fields)
        for blocks in (range(NEAR, NBK), range(NEAR)):
            o = mm(lhs, esel[:, blocks[0] * HB : (blocks[-1] + 1) * HB])
            for i, slot in enumerate(slots):
                values = fold(o, i)
                for b in blocks:
                    snd[slot, b] = values[:, (b - blocks[0]) * HB : (b - blocks[0] + 1) * HB]
            if slots[0] == 6:
                if blocks[0] == NEAR:
                    continue
                pl.semaphore_wait(barrier, len(peers))
                blocks = SEND_ORDER
            for slot in slots:
                for b in blocks:
                    halo_copy(slot, b).start()

    def arrived(slot, far):
        part = rcv.at[slot, pl.ds(NEAR, NBK - NEAR)] if far else rcv.at[slot, pl.ds(0, NEAR)]
        pltpu.make_async_copy(part, part, s_recv.at[slot, int(far)]).wait()
        blocks = range(NEAR, NBK) if far else range(NEAR)
        return rows2(jnp.concatenate([rcv[slot, b] for b in blocks], axis=1))

    loaded(1)
    theta = t_in[...]
    pres = p_in[...]
    export_and_send(6, theta, 0, pres)

    er = lax.broadcasted_iota(jnp.int32, (3 * HB, 3 * HB), 0)
    ec = lax.broadcasted_iota(jnp.int32, (3 * HB, 3 * HB), 1)
    order = jnp.where(er == 3 * (ec % HB) + ec // HB, 1.0, 0.0).astype(F32).astype(BF16).astype(F8)
    loaded(2)
    ends = end_in[1:2, :]
    smalls = [(ends // 256).astype(F32), (ends % 256).astype(F32)]
    smalls += [part.astype(F32) for row in (len_in, met_in) for part in split3(row[...])]
    smalls = jnp.concatenate(smalls + [jnp.zeros((8, 3 * CC), F32)], axis=0).astype(BF16)
    loaded(3)
    speed = par[0, 0]
    kappa = 0.5 * par[0, 1]
    mixing = 0.6 * par[0, 2]
    couple = par[0, 3]
    inv = inv_in[...]
    stacked = jnp.concatenate([rows2(v_in[...]), smalls], axis=0)
    for g in range(CC // HB):
        o = mm(stacked[:, g * 3 * HB : (g + 1) * 3 * HB], order)
        vel = fold(o)
        small = jnp.concatenate(
            [o[64:65], o[65:66], o[66:67] + o[67:68] + o[68:69], o[69:70] + o[70:71] + o[71:72], o[76:80]], axis=0
        )
        for j in range(3):
            vd[j, :, g * HB : (g + 1) * HB] = vel[:, j * HB : (j + 1) * HB]
            sd[j, :, g * HB : (g + 1) * HB] = small[:, j * HB : (j + 1) * HB]

    owned = sd[0, 0:1, :] < EXT // 256

    def build(t, carry):
        base = pl.multiple_of(t * 256, 256)
        tf = t.astype(F32)
        for g in range(CC // HB):
            lanes = slice(g * HB, (g + 1) * HB)
            for j in range(3):
                want = packed_row((sd[j, 0:1, lanes] - tf) * 256.0 + sd[j, 1:2, lanes])
                for r in range(8):
                    sel[j, pl.ds(base + 32 * r, 32), lanes] = hot(r, want)
        return carry

    lax.fori_loop(0, EXT // 256, build, 0)

    def coefficients(j):
        v = vd[j]
        length = sd[j, 2:3, :]
        return length * (jnp.maximum(v, 0.0) + kappa), length * (jnp.minimum(v, 0.0) - kappa)

    def weight(j):
        return sd[j, 3:4, :]

    def near_both(p, th):
        lhs = rows2(p, th)
        net_p, net_t = jnp.zeros((LV, CC), F32), jnp.zeros((LV, CC), F32)
        for j in range(3):
            ends_of = mm(lhs, sel[j, :CC, :])
            start, end = coefficients(j)
            grad = weight(j) * (fold(ends_of, 0) - p)
            flux = start * th + end * fold(ends_of, 1)
            incoming = mm_t(rows2(grad, flux), sel[j, :CC, :])
            net_p = net_p + grad - fold(incoming, 0)
            net_t = net_t + flux - fold(incoming, 1)
        return net_p, net_t

    def near_pressure(p):
        lhs = rows2(p)
        net = jnp.zeros((LV, CC), F32)
        for j in range(3):
            grad = weight(j) * (fold(mm(lhs, sel[j, :CC, :])) - p)
            net = net + grad - fold(mm_t(rows2(grad), sel[j, :CC, :]))
        return net

    def far_part(slot, scales, net):
        split = CC + NEAR * HB
        lhs = arrived(slot, False)
        for j in range(3):
            net = net + scales[j] * fold(mm(lhs, sel[j, CC:split, :]))
        lhs = arrived(slot, True)
        for j in range(3):
            net = net + scales[j] * fold(mm(lhs, sel[j, split:, :]))
        return net

    def far_pressure(slot, net):
        return far_part(slot, [weight(j) for j in range(3)], net)

    def far_theta(slot, net):
        return far_part(slot, [coefficients(j)[1] for j in range(3)], net)

    def advance_theta(th, net):
        up = jnp.concatenate([th[1:], th[LV - 1 :]], axis=0) - th
        down = th - jnp.concatenate([th[:1], th[: LV - 1]], axis=0)
        return jnp.where(owned, th + DT * (mixing * (up - down) - inv * net), th)

    scale = speed * inv

    def advance(p, q, net, force):
        return jnp.where(owned, 2.0 * p - q + scale * net + force, p), p

    area = jnp.where(owned, 1.0 / inv, 0.0)

    def by_lane(p, factor):
        return sum(
            p[:, g * HB : (g + 1) * HB] * factor[:, g * HB : (g + 1) * HB] for g in range(CC // HB)
        )

    def partial_row(total):
        spread = by_lane(jnp.ones((1, CC), F32), area)
        padded = jnp.concatenate([total, spread, jnp.zeros((HB - LV - 1, HB), F32)], axis=0)
        return jnp.sum(padded.T, axis=0, keepdims=True)

    def reach_copy(b):
        return pltpu.make_async_remote_copy(
            src_ref=reach.at[b],
            dst_ref=reach_in.at[b],
            send_sem=h_sem.at[0],
            recv_sem=h_sem.at[1],
            device_id=(m, (d - OFFSETS[b] + n_dom) % n_dom),
            device_id_type=MESH,
        )

    def send_reach():
        total = jnp.zeros((16, HALO), F32)
        for j in range(3):
            parts = jnp.concatenate([part.astype(F32) for part in split3(weight(j))] + [jnp.zeros((13, CC), F32)], axis=0)
            total = total + mm_t(parts.astype(BF16), sel[j, CC:, :])
        total = jnp.sum(total, axis=0, keepdims=True)
        for b in range(NBK):
            reach[b] = total[:, b * HB : (b + 1) * HB]
            reach_copy(b).start()

    def next_total(slot, p, q, force):
        pltpu.make_async_copy(reach_in, reach_in, h_sem.at[1]).wait()
        leaving = jnp.zeros((1, CC), F32)
        for j in range(3):
            block = sd[j, 0:1, :]
            leaving = leaving + jnp.where((block >= CC // 256) & (block < EXT // 256), weight(j), 0.0)
        total = by_lane(2.0 * p - q + force, area) - speed * by_lane(p, leaving)
        for b in range(NBK):
            total = total + speed * (snd[slot, b] * reach_in[b])
        return total

    def spread_row(row):
        return jnp.broadcast_to(row, (HB, HB)).T[:LV]

    def line_copy(which, k):
        return pltpu.make_async_remote_copy(
            src_ref=row_a.at[which],
            dst_ref=box_a.at[which, pos],
            send_sem=a_send,
            recv_sem=a_recv.at[which],
            device_id=in_line[k],
            device_id_type=MESH,
        )

    def wide_copy(which, n):
        return pltpu.make_async_remote_copy(
            src_ref=row_b.at[which],
            dst_ref=box_x.at[which, m * n_line + line],
            send_sem=b_send,
            recv_sem=b_recv.at[which],
            device_id=across[n],
            device_id_type=MESH,
        )

    def start_mean(which, total):
        row = partial_row(total)
        row_a[which] = row
        for k in range(LINE - 1):
            line_copy(which, k).start()
        box_a[which, pos] = row

    def turn_mean(which):
        others = box_a.at[which, pl.ds(0, LINE - 1)]
        pltpu.make_async_copy(others, others, a_recv.at[which]).wait()
        row = jnp.sum(box_a[which], axis=0)
        row_b[which] = row
        for n in range(len(shifts)):
            wide_copy(which, n).start()
        box_x[which, m * n_line + line] = row

    def end_mean(which):
        others = box_x.at[which, pl.ds(0, len(shifts))]
        pltpu.make_async_copy(others, others, b_recv.at[which]).wait()

    def mean_of(which, member):
        return level_mean(box_x[which, pl.ds(member * n_line, n_line)])

    def level_mean(rows):
        row = jnp.sum(rows, axis=0)
        return row / row[:, LV : LV + 1]

    def less_mean(p, mean):
        wide = jnp.concatenate([spread_row(mean)] * (CC // HB), axis=1)
        return p - jnp.where(owned, wide, 0.0)

    net, net_theta = near_both(pres, theta)
    theta_next = advance_theta(theta, far_theta(6, net_theta))
    force = couple * (theta_next - theta) / NS
    theta = theta_next
    pres, prev = advance(pres, q_in[...], far_pressure(0, net), force)
    export_and_send(1, pres)
    export_and_send(7, theta)
    net = near_pressure(pres)
    send_reach()
    pres, prev = advance(pres, prev, far_pressure(1, net), force)
    export_and_send(2, pres)
    net, net_theta = near_both(pres, theta)
    pres, prev = advance(pres, prev, far_pressure(2, net), force)
    export_and_send(3, pres)
    start_mean(0, by_lane(pres, area))
    net = near_pressure(pres)
    theta_next = advance_theta(theta, far_theta(7, net_theta))
    force = couple * (theta_next - theta) / NS
    t_out[...] = theta_next
    pres, prev = advance(pres, prev, far_pressure(3, net), force)
    export_and_send(4, pres)
    net = near_pressure(pres)
    turn_mean(0)
    pres, prev = advance(pres, prev, far_pressure(4, net), force)
    export_and_send(5, pres)
    start_mean(1, next_total(5, pres, prev, force))
    net = near_pressure(pres)
    end_mean(0)
    pres, prev = advance(pres, prev, far_pressure(5, net), force)
    current = less_mean(pres, mean_of(0, m))
    cur_buf[...] = current

    band = LV // n_mem

    def scatter_copy(k):
        peer = (m + k) % n_mem
        return pltpu.make_async_remote_copy(
            src_ref=cur_buf.at[pl.ds(pl.multiple_of(peer * band, band), band), :],
            dst_ref=rs_box.at[m],
            send_sem=x_send.at[0],
            recv_sem=x_recv.at[0],
            device_id=(peer, d),
            device_id_type=MESH,
        )

    def gather_copy(k):
        return pltpu.make_async_remote_copy(
            src_ref=slab,
            dst_ref=ens.at[m],
            send_sem=x_send.at[1],
            recv_sem=x_recv.at[1],
            device_id=((m + k) % n_mem, d),
            device_id_type=MESH,
        )

    steps = sorted(range(1, n_mem), key=lambda k: -min(k, n_mem - k))
    for k in steps:
        scatter_copy(k).start()
    rs_box[m] = cur_buf[pl.ds(pl.multiple_of(m * band, band), band), :]
    turn_mean(1)
    others = rs_box.at[pl.ds(0, n_mem - 1)]
    pltpu.make_async_copy(others, others, x_recv.at[0]).wait()
    total = jnp.sum(rs_box[...], axis=0)
    slab[...] = total
    for k in steps:
        gather_copy(k).start()
    ens[m] = total
    end_mean(1)
    p_out[...] = less_mean(current, mean_of(1, m) - mean_of(0, m))
    all_means = mean_of(1, 0) - mean_of(0, 0)
    for i in range(1, n_mem):
        all_means = all_means + (mean_of(1, i) - mean_of(0, i))
    others = ens.at[pl.ds(0, n_mem - 1)]
    pltpu.make_async_copy(others, others, x_recv.at[1]).wait()
    summed = jnp.concatenate([ens[i] for i in range(n_mem)], axis=0)
    e_out[...] = less_mean(summed, all_means) / n_mem

    pltpu.make_async_copy(snd, snd, s_send).wait()
    pltpu.make_async_copy(reach, reach, h_sem.at[0]).wait()
    sent = box_a.at[:, pl.ds(0, LINE - 1)]
    pltpu.make_async_copy(sent, sent, a_send).wait()
    sent = box_x.at[:, pl.ds(0, len(shifts))]
    pltpu.make_async_copy(sent, sent, b_send).wait()
    sent = ens.at[pl.ds(0, n_mem - 1)]
    for phase in range(2):
        pltpu.make_async_copy(sent, sent, x_send.at[phase]).wait()


def hand_over(p, t, e, p_out, t_out, e_out, sem):
    moves = [
        pltpu.make_async_copy(src, dst, sem.at[i])
        for i, (src, dst) in enumerate(((p, p_out.at[0]), (t, t_out.at[0]), (e, e_out)))
    ]
    for move in moves:
        move.start()
    for move in moves:
        move.wait()


def per_device(
    acoustic_perturbation,
    prior_acoustic_state,
    thermal_anomaly,
    model_parameters,
    crossing_velocity,
    face_extent,
    face_metric_factor,
    reciprocal_polygon_surface,
    owned_totals,
    export_lists,
    face_neighbour_pair,
    polygon_side_lookup,
):
    n_mem = lax.axis_size("member")
    n_line = lax.axis_size("dom") // LINE
    n_all = n_mem * n_line
    band = LV // n_mem
    vmem = pl.BlockSpec(memory_space=pltpu.VMEM)
    anyw = pl.BlockSpec(memory_space=pl.ANY)
    dma = pltpu.SemaphoreType.DMA
    held = pl.pallas_call(
        kernel,
        out_shape=tuple(pltpu.VMEM((LV, CC), F32) for _ in range(3)),
        in_specs=[anyw] * 10,
        out_specs=(vmem, vmem, vmem),
        scratch_shapes=[
            pltpu.SMEM((1, 4), F32),
            pltpu.VMEM((LV, CC), F32),
            pltpu.VMEM((LV, CC), F32),
            pltpu.VMEM((LV, CC), F32),
            pltpu.VMEM((LV, 3 * CC), F32),
            pltpu.VMEM((1, 3 * CC), F32),
            pltpu.VMEM((1, 3 * CC), F32),
            pltpu.VMEM((1, CC), F32),
            pltpu.VMEM((NBK, 1, HB), jnp.int32),
            pltpu.VMEM((2, 3 * CC), jnp.int32),
            pltpu.VMEM((3, EXT, CC), F8),
            pltpu.VMEM((CC, HALO), F8),
            pltpu.VMEM((3, LV, CC), F32),
            pltpu.VMEM((3, 8, CC), F32),
            pltpu.VMEM((8, NBK, LV, HB), F32),
            pltpu.VMEM((8, NBK, LV, HB), F32),
            pltpu.VMEM((NBK, 1, HB), F32),
            pltpu.VMEM((NBK, 1, HB), F32),
            pltpu.VMEM((2, 1, HB), F32),
            pltpu.VMEM((2, 1, HB), F32),
            pltpu.VMEM((2, LINE, 1, HB), F32),
            pltpu.VMEM((2, n_all, 1, HB), F32),
            pltpu.VMEM((LV, CC), F32),
            pltpu.VMEM((n_mem, band, CC), F32),
            pltpu.VMEM((band, CC), F32),
            pltpu.VMEM((n_mem, band, CC), F32),
            dma((10,)),
            dma,
            dma((8, 2)),
            dma((2,)),
            dma,
            dma((2,)),
            dma,
            dma((2,)),
            dma((2,)),
            dma((2,)),
        ],
        compiler_params=pltpu.CompilerParams(collective_id=0, has_side_effects=True),
    )(
        model_parameters,
        acoustic_perturbation,
        prior_acoustic_state,
        thermal_anomaly,
        crossing_velocity,
        face_extent[None, :],
        face_metric_factor[None, :],
        reciprocal_polygon_surface[None, :],
        export_lists.reshape(NBK, 1, HB),
        face_neighbour_pair,
    )
    return pl.pallas_call(
        hand_over,
        out_shape=(
            jax.ShapeDtypeStruct((1, LV, CC), F32),
            jax.ShapeDtypeStruct((1, LV, CC), F32),
            jax.ShapeDtypeStruct((LV, CC), F32),
        ),
        in_specs=[vmem] * 3,
        out_specs=(anyw, anyw, anyw),
        scratch_shapes=[dma((3,))],
    )(*[pltpu.with_memory_space_constraint(x, pltpu.VMEM) for x in held])


def solution(mesh):
    in_specs = (
        P("member", None, "dom"),
        P("member", None, "dom"),
        P("member", None, "dom"),
        P("member", None),
        P(None, "dom"),
        P("dom"),
        P("dom"),
        P("dom"),
        P("dom"),
        P("dom", None, None),
        P(None, "dom"),
        P(None, "dom"),
    )
    out_specs = (P("member", None, "dom"), P("member", None, "dom"), P(None, "dom"))
    return jax.shard_map(
        per_device, mesh=mesh, in_specs=in_specs, out_specs=out_specs, check_vma=False
    )
```

time: 56.3 us -> 52.7 us (0.936)
  Pallas kernels: 54.8 us -> 51.5 us
  between operations: 1.29 us -> 0.64 us
    pallas_call x1, Pallas kernels: 54.1 us -> 50.7 us  [per_device(): pl.pallas_call(kernel, out_shape=tuple((pltpu.VMEM((LV, CC), F32) for _ i...]
where the time goes in v3:
time: 52.7 us; the launch traced here: 52.1 us
  Pallas kernels  51.5 us (98%)
  between operations  0.64 us (1%)
    pallas_call x1, Pallas kernels, per_device(): pl.pallas_call(kernel, out_shape=tuple((pltpu.VMEM((LV, CC), F32) for _ i...  50.7 us

profile of v3, /device:TPU:1, one launch (start us, length us, event | category | flops | bytes accessed | tf_op | source)
XLA Modules:
  0.0 52.1 jit_solution(12726058745777686825)
XLA Ops:
  0.6 50.7 %shard_map.121 = (f32[32,1024]{1,0:T(8,128)S(1)}, f32[32,1024]{1,0:T(8,128)S(1)}, f32[32,1024]{1,0:T(8,128)S(1)}) custom-call(f32[1,4]{1,0:T(1,128)} %par_hbm.1, f32[1,32,1024]{2,1,0:T(8,128)} %p_hbm.1, f32[1,32,1024]{2,1,0:T(8,128)} %q_hbm.1, f32[1,32,1024]{2,1,0:T(8,128)} %t_hbm.1, f32[32,3072]{1,0:T(8,128)} %v_hbm.1, f32[1,3072]{1,0:T(1,128)} %bitcast.4, ...), custom_call_target="tpu_custom_call" | custom-call | tf_op jit(solution)/shard_map/pallas_call | solution.py:468
  51.3 0.8 %shard_map.122 = (f32[1,32,1024]{2,1,0:T(8,128)}, f32[1,32,1024]{2,1,0:T(8,128)}, f32[32,1024]{1,0:T(8,128)}) custom-call(f32[32,1024]{1,0:T(8,128)S(1)} %get-tuple-element.6.p, f32[32,1024]{1,0:T(8,128)S(1)} %get-tuple-element.7.t, f32[32,1024]{1,0:T(8,128)S(1)} %get-tuple-element.8.e), custom_call_target="tpu_custom_call" | custom-call | tf_op jit(solution)/shard_map/pallas_call | solution.py:524

commit v4 on v3

--- a/solution.py
+++ b/solution.py
@@ -21,7 +21,6 @@
 NS = 3
 OFFSETS = [(b // 2 + 1) * (1 - 2 * (b % 2)) for b in range(NBK)]
 SEND_ORDER = (4, 5, 2, 3, 0, 1)
-NEAR = 4
 
 
 def split2(x):
@@ -58,8 +57,8 @@
     par_hbm, p_hbm, q_hbm, t_hbm, v_hbm, len_hbm, met_hbm, inv_hbm, exp_hbm, end_hbm,
     p_out, t_out, e_out,
     par, p_in, q_in, t_in, v_in, len_in, met_in, inv_in, exp_in, end_in,
-    sel, esel, vd, sd, snd, rcv, reach, reach_in, row_a, row_b, box_a, box_x, cur_buf, rs_box, slab, ens,
-    in_sem, s_send, s_recv, h_sem, a_send, a_recv, b_send, b_recv, x_send, x_recv,
+    sel, esel, vd, sd, snd, rcv, reach, reach_in, row_a, row_b, box_a, box_x, zsnd, zbox, cur_buf, rs_box, slab, ens,
+    in_sem, s_send, s_recv, h_send, h_recv, z_send, z_recv, a_send, a_recv, b_send, b_recv, x_send, x_recv,
 ):
     n_mem = lax.axis_size("member")
     n_dom = lax.axis_size("dom")
@@ -67,16 +66,6 @@
     m = lax.axis_index("member")
     d = lax.axis_index("dom")
     line, pos = d // LINE, d % LINE
-
-    neighbours = [(m, (d + off + n_dom) % n_dom) for off in OFFSETS]
-    in_line = [(m, line * LINE + (pos + k) % LINE) for k in range(1, LINE)]
-    shifts = [(i, k) for i in range(n_mem) for k in range(n_line) if i or k]
-    across = [((m + i) % n_mem, (d + k * LINE) % n_dom) for i, k in shifts]
-
-    barrier = pltpu.get_barrier_semaphore()
-    peers = neighbours + in_line + across
-    for peer in peers:
-        pl.semaphore_signal(barrier, inc=1, device_id=peer, device_id_type=MESH)
 
     sources = (exp_hbm, t_hbm.at[0], p_hbm.at[0], end_hbm, len_hbm, met_hbm, v_hbm, inv_hbm, par_hbm, q_hbm.at[0])
     targets = (exp_in, t_in, p_in, end_in, len_in, met_in, v_in, inv_in, par, q_in)
@@ -87,6 +76,17 @@
     for load in loads:
         load.start()
 
+    neighbours = [(m, (d + off + n_dom) % n_dom) for off in OFFSETS]
+    in_line = [(m, line * LINE + (pos + k) % LINE) for k in range(1, LINE)]
+    shifts = [(i, k) for i in range(n_mem) for k in range(n_line) if i or k]
+    across = [((m + i) % n_mem, (d + k * LINE) % n_dom) for i, k in shifts]
+
+    barrier = pltpu.get_barrier_semaphore()
+    peers = neighbours + in_line + across
+    peers += [((m + i) % n_mem, p) for i in range(1, n_mem) for _, p in neighbours]
+    for peer in peers:
+        pl.semaphore_signal(barrier, inc=1, device_id=peer, device_id_type=MESH)
+
     def loaded(group):
         for load, its in zip(loads, groups):
             if its == group:
@@ -102,6 +102,9 @@
     def hot(r, want):
         return jnp.where(iota32 + jnp.asarray(32.0 * r, BF16) == want, one, zero).astype(F8)
 
+    er = lax.broadcasted_iota(jnp.int32, (3 * HB, 3 * HB), 0)
+    ec = lax.broadcasted_iota(jnp.int32, (3 * HB, 3 * HB), 1)
+    order = jnp.where(er == 3 * (ec % HB) + ec // HB, 1.0, 0.0).astype(F32).astype(BF16).astype(F8)
     loaded(0)
 
     def build_exports(t, carry):
@@ -119,43 +122,34 @@
             src_ref=snd.at[slot, b],
             dst_ref=rcv.at[slot, b],
             send_sem=s_send,
-            recv_sem=s_recv.at[slot, b // NEAR],
+            recv_sem=s_recv.at[slot],
             device_id=neighbours[b],
             device_id_type=MESH,
         )
 
     def export_and_send(*slots_and_fields):
         slots, fields = slots_and_fields[::2], slots_and_fields[1::2]
-        lhs = rows2(*fields)
-        for blocks in (range(NEAR, NBK), range(NEAR)):
-            o = mm(lhs, esel[:, blocks[0] * HB : (blocks[-1] + 1) * HB])
-            for i, slot in enumerate(slots):
-                values = fold(o, i)
-                for b in blocks:
-                    snd[slot, b] = values[:, (b - blocks[0]) * HB : (b - blocks[0] + 1) * HB]
-            if slots[0] == 6:
-                if blocks[0] == NEAR:
-                    continue
-                pl.semaphore_wait(barrier, len(peers))
-                blocks = SEND_ORDER
-            for slot in slots:
-                for b in blocks:
-                    halo_copy(slot, b).start()
-
-    def arrived(slot, far):
-        part = rcv.at[slot, pl.ds(NEAR, NBK - NEAR)] if far else rcv.at[slot, pl.ds(0, NEAR)]
-        pltpu.make_async_copy(part, part, s_recv.at[slot, int(far)]).wait()
-        blocks = range(NEAR, NBK) if far else range(NEAR)
-        return rows2(jnp.concatenate([rcv[slot, b] for b in blocks], axis=1))
+        o = mm(rows2(*fields), esel[...])
+        for i, slot in enumerate(slots):
+            values = fold(o, i)
+            for b in range(NBK):
+                snd[slot, b] = values[:, b * HB : (b + 1) * HB]
+        if slots[0] == 6:
+            pl.semaphore_wait(barrier, len(peers))
+        for slot in slots:
+            for b in SEND_ORDER:
+                halo_copy(slot, b).start()
+        return fold(o)
+
+    def arrived(slot):
+        pltpu.make_async_copy(rcv.at[slot], rcv.at[slot], s_recv.at[slot]).wait()
+        return jnp.concatenate([rcv[slot, b] for b in range(NBK)], axis=1)
 
     loaded(1)
     theta = t_in[...]
     pres = p_in[...]
     export_and_send(6, theta, 0, pres)
 
-    er = lax.broadcasted_iota(jnp.int32, (3 * HB, 3 * HB), 0)
-    ec = lax.broadcasted_iota(jnp.int32, (3 * HB, 3 * HB), 1)
-    order = jnp.where(er == 3 * (ec % HB) + ec // HB, 1.0, 0.0).astype(F32).astype(BF16).astype(F8)
     loaded(2)
     ends = end_in[1:2, :]
     smalls = [(ends // 256).astype(F32), (ends % 256).astype(F32)]
@@ -180,18 +174,19 @@
 
     owned = sd[0, 0:1, :] < EXT // 256
 
-    def build(t, carry):
-        base = pl.multiple_of(t * 256, 256)
-        tf = t.astype(F32)
+    def build_tile(t, tf, base):
         for g in range(CC // HB):
             lanes = slice(g * HB, (g + 1) * HB)
             for j in range(3):
                 want = packed_row((sd[j, 0:1, lanes] - tf) * 256.0 + sd[j, 1:2, lanes])
                 for r in range(8):
                     sel[j, pl.ds(base + 32 * r, 32), lanes] = hot(r, want)
+
+    def build(t, carry):
+        build_tile(t, t.astype(F32), pl.multiple_of(t * 256, 256))
         return carry
 
-    lax.fori_loop(0, EXT // 256, build, 0)
+    lax.fori_loop(0, CC // 256, build, 0)
 
     def coefficients(j):
         v = vd[j]
@@ -201,42 +196,52 @@
     def weight(j):
         return sd[j, 3:4, :]
 
-    def near_both(p, th):
-        lhs = rows2(p, th)
-        net_p, net_t = jnp.zeros((LV, CC), F32), jnp.zeros((LV, CC), F32)
+    def near(*fields, theta_last=False):
+        spans, at = [], 0
+        for field in fields:
+            spans.append((at, field.shape[0]))
+            at += 2 * field.shape[0]
+
+        def part(o, i):
+            first, rows = spans[i]
+            return o[first : first + rows] + o[first + rows : first + 2 * rows]
+
+        lhs = rows2(*fields)
+        nets = [jnp.zeros_like(field) for field in fields]
+        ends_of = [mm(lhs, sel[0, :CC, :]), None, None]
         for j in range(3):
-            ends_of = mm(lhs, sel[j, :CC, :])
-            start, end = coefficients(j)
-            grad = weight(j) * (fold(ends_of, 0) - p)
-            flux = start * th + end * fold(ends_of, 1)
-            incoming = mm_t(rows2(grad, flux), sel[j, :CC, :])
-            net_p = net_p + grad - fold(incoming, 0)
-            net_t = net_t + flux - fold(incoming, 1)
+            if j < 2:
+                ends_of[j + 1] = mm(lhs, sel[j + 1, :CC, :])
+            flows = []
+            for i, field in enumerate(fields):
+                if theta_last and i == len(fields) - 1:
+                    start, end = coefficients(j)
+                    flows.append(start * field + end * part(ends_of[j], i))
+                else:
+                    flows.append(weight(j) * (part(ends_of[j], i) - field))
+            incoming = mm_t(rows2(*flows), sel[j, :CC, :])
+            nets = [net + flow - part(incoming, i) for i, (net, flow) in enumerate(zip(nets, flows))]
+        return nets
+
+    def far_pressure(slot, net):
+        lhs = rows2(arrived(slot))
+        for j in range(3):
+            net = net + weight(j) * fold(mm(lhs, sel[j, CC:, :]))
+        return net
+
+    def far_theta(slot, net):
+        lhs = rows2(arrived(slot))
+        for j in range(3):
+            net = net + coefficients(j)[1] * fold(mm(lhs, sel[j, CC:, :]))
+        return net
+
+    def far_both(slot_p, net_p, slot_t, net_t):
+        lhs = rows2(arrived(slot_p), arrived(slot_t))
+        for j in range(3):
+            o = mm(lhs, sel[j, CC:, :])
+            net_p = net_p + weight(j) * fold(o, 0)
+            net_t = net_t + coefficients(j)[1] * fold(o, 1)
         return net_p, net_t
-
-    def near_pressure(p):
-        lhs = rows2(p)
-        net = jnp.zeros((LV, CC), F32)
-        for j in range(3):
-            grad = weight(j) * (fold(mm(lhs, sel[j, :CC, :])) - p)
-            net = net + grad - fold(mm_t(rows2(grad), sel[j, :CC, :]))
-        return net
-
-    def far_part(slot, scales, net):
-        split = CC + NEAR * HB
-        lhs = arrived(slot, False)
-        for j in range(3):
-            net = net + scales[j] * fold(mm(lhs, sel[j, CC:split, :]))
-        lhs = arrived(slot, True)
-        for j in range(3):
-            net = net + scales[j] * fold(mm(lhs, sel[j, split:, :]))
-        return net
-
-    def far_pressure(slot, net):
-        return far_part(slot, [weight(j) for j in range(3)], net)
-
-    def far_theta(slot, net):
-        return far_part(slot, [coefficients(j)[1] for j in range(3)], net)
 
     def advance_theta(th, net):
         up = jnp.concatenate([th[1:], th[LV - 1 :]], axis=0) - th
@@ -260,36 +265,37 @@
         padded = jnp.concatenate([total, spread, jnp.zeros((HB - LV - 1, HB), F32)], axis=0)
         return jnp.sum(padded.T, axis=0, keepdims=True)
 
-    def reach_copy(b):
+    def reach_copy(which, b):
         return pltpu.make_async_remote_copy(
-            src_ref=reach.at[b],
-            dst_ref=reach_in.at[b],
-            send_sem=h_sem.at[0],
-            recv_sem=h_sem.at[1],
+            src_ref=reach.at[which, b],
+            dst_ref=reach_in.at[which, b],
+            send_sem=h_send,
+            recv_sem=h_recv.at[which],
             device_id=(m, (d - OFFSETS[b] + n_dom) % n_dom),
             device_id_type=MESH,
         )
 
-    def send_reach():
+    def three_rows(row):
+        parts = [part.astype(F32) for part in split3(row)]
+        return jnp.concatenate(parts + [jnp.zeros((13, row.shape[1]), F32)], axis=0).astype(BF16)
+
+    def send_reach(which, rows):
         total = jnp.zeros((16, HALO), F32)
         for j in range(3):
-            parts = jnp.concatenate([part.astype(F32) for part in split3(weight(j))] + [jnp.zeros((13, CC), F32)], axis=0)
-            total = total + mm_t(parts.astype(BF16), sel[j, CC:, :])
+            total = total + mm_t(three_rows(rows[j]), sel[j, CC:, :])
         total = jnp.sum(total, axis=0, keepdims=True)
         for b in range(NBK):
-            reach[b] = total[:, b * HB : (b + 1) * HB]
-            reach_copy(b).start()
-
-    def next_total(slot, p, q, force):
-        pltpu.make_async_copy(reach_in, reach_in, h_sem.at[1]).wait()
-        leaving = jnp.zeros((1, CC), F32)
-        for j in range(3):
-            block = sd[j, 0:1, :]
-            leaving = leaving + jnp.where((block >= CC // 256) & (block < EXT // 256), weight(j), 0.0)
-        total = by_lane(2.0 * p - q + force, area) - speed * by_lane(p, leaving)
-        for b in range(NBK):
-            total = total + speed * (snd[slot, b] * reach_in[b])
-        return total
+            reach[which, b] = total[:, b * HB : (b + 1) * HB]
+            reach_copy(which, b).start()
+
+    def reached(which):
+        pltpu.make_async_copy(reach_in.at[which], reach_in.at[which], h_recv.at[which]).wait()
+        row = jnp.concatenate([reach_in[which, b] for b in range(NBK)], axis=1)
+        return jnp.sum(mm_t(three_rows(row), esel[...]), axis=0, keepdims=True)
+
+    def halo_weight(j):
+        block = sd[j, 0:1, :]
+        return jnp.where((block >= CC // 256) & (block < EXT // 256), weight(j), 0.0)
 
     def spread_row(row):
         return jnp.broadcast_to(row, (HB, HB)).T[:LV]
@@ -341,48 +347,66 @@
         row = jnp.sum(rows, axis=0)
         return row / row[:, LV : LV + 1]
 
-    def less_mean(p, mean):
-        wide = jnp.concatenate([spread_row(mean)] * (CC // HB), axis=1)
-        return p - jnp.where(owned, wide, 0.0)
-
-    net, net_theta = near_both(pres, theta)
-    theta_next = advance_theta(theta, far_theta(6, net_theta))
+    def over_cells(mean):
+        return jnp.where(owned, jnp.concatenate([spread_row(mean)] * (CC // HB), axis=1), 0.0)
+
+    for t in range(CC // 256, EXT // 256):
+        build_tile(t, float(t), t * 256)
+    net, net_theta = near(pres, theta, theta_last=True)
+    net, net_theta = far_both(0, net, 6, net_theta)
+    theta_next = advance_theta(theta, net_theta)
     force = couple * (theta_next - theta) / NS
     theta = theta_next
-    pres, prev = advance(pres, q_in[...], far_pressure(0, net), force)
+    pres, prev = advance(pres, q_in[...], net, force)
     export_and_send(1, pres)
     export_and_send(7, theta)
-    net = near_pressure(pres)
-    send_reach()
+    send_reach(0, [weight(j) for j in range(3)])
+    (net,) = near(pres)
     pres, prev = advance(pres, prev, far_pressure(1, net), force)
     export_and_send(2, pres)
-    net, net_theta = near_both(pres, theta)
+    net, net_theta = near(pres, theta, theta_last=True)
+    once = reached(0) - halo_weight(0) - halo_weight(1) - halo_weight(2)
+    scaled = jnp.where(owned, once * inv, 0.0)
+    send_reach(1, [weight(j) * scaled for j in range(3)])
     pres, prev = advance(pres, prev, far_pressure(2, net), force)
     export_and_send(3, pres)
     start_mean(0, by_lane(pres, area))
-    net = near_pressure(pres)
+    net, twice = near(pres, jnp.concatenate([scaled, jnp.zeros((7, CC), F32)], axis=0))
+    twice = twice[0:1] + reached(1)
     theta_next = advance_theta(theta, far_theta(7, net_theta))
     force = couple * (theta_next - theta) / NS
     t_out[...] = theta_next
+    by_p = 3.0 * area + speed * (4.0 * once + speed * twice)
+    by_q = 2.0 * area + speed * once
+    by_f = 3.0 * area + speed * once
     pres, prev = advance(pres, prev, far_pressure(3, net), force)
     export_and_send(4, pres)
-    net = near_pressure(pres)
+    start_mean(1, by_lane(pres, by_p) - by_lane(prev, by_q) + by_lane(force, by_f))
+    (net,) = near(pres)
     turn_mean(0)
     pres, prev = advance(pres, prev, far_pressure(4, net), force)
-    export_and_send(5, pres)
-    start_mean(1, next_total(5, pres, prev, force))
-    net = near_pressure(pres)
-    end_mean(0)
-    pres, prev = advance(pres, prev, far_pressure(5, net), force)
-    current = less_mean(pres, mean_of(0, m))
-    cur_buf[...] = current
 
     band = LV // n_mem
+    steps = sorted(range(1, n_mem), key=lambda k: -min(k, n_mem - k))
+
+    def band_of(member):
+        return pl.ds(pl.multiple_of(member * band, band), band)
+
+    def sum_copy(k, b):
+        peer = (m + k) % n_mem
+        return pltpu.make_async_remote_copy(
+            src_ref=zsnd.at[b, band_of(peer), :],
+            dst_ref=zbox.at[m, b],
+            send_sem=z_send,
+            recv_sem=z_recv,
+            device_id=(peer, neighbours[b][1]),
+            device_id_type=MESH,
+        )
 
     def scatter_copy(k):
         peer = (m + k) % n_mem
         return pltpu.make_async_remote_copy(
-            src_ref=cur_buf.at[pl.ds(pl.multiple_of(peer * band, band), band), :],
+            src_ref=cur_buf.at[band_of(peer), :],
             dst_ref=rs_box.at[m],
             send_sem=x_send.at[0],
             recv_sem=x_recv.at[0],
@@ -400,30 +424,56 @@
             device_id_type=MESH,
         )
 
-    steps = sorted(range(1, n_mem), key=lambda k: -min(k, n_mem - k))
+    values = speed * export_and_send(5, pres)
+    for b in range(NBK):
+        zsnd[b] = values[:, b * HB : (b + 1) * HB]
+    for k in steps:
+        for b in SEND_ORDER:
+            sum_copy(k, b).start()
+    (net,) = near(pres)
+    cur_buf[...] = advance(pres, prev, net, force)[0]
     for k in steps:
         scatter_copy(k).start()
-    rs_box[m] = cur_buf[pl.ds(pl.multiple_of(m * band, band), band), :]
+    rs_box[m] = cur_buf[band_of(m), :]
     turn_mean(1)
+    far = far_pressure(5, jnp.zeros((LV, CC), F32))
+    for b in range(NBK):
+        zbox[m, b] = speed * rcv[5, b, band_of(m), :]
     others = rs_box.at[pl.ds(0, n_mem - 1)]
     pltpu.make_async_copy(others, others, x_recv.at[0]).wait()
-    total = jnp.sum(rs_box[...], axis=0)
+    others = zbox.at[pl.ds(0, n_mem - 1)]
+    pltpu.make_async_copy(others, others, z_recv).wait()
+    lhs = rows2(jnp.sum(jnp.concatenate([zbox[:, b] for b in range(NBK)], axis=2), axis=0))
+    total = jnp.zeros((band, CC), F32)
+    for j in range(3):
+        o = mm(lhs, sel[j, CC:, :])
+        total = total + weight(j) * (o[:band] + o[band:])
+    total = jnp.sum(rs_box[...], axis=0) + jnp.where(owned, inv * total, 0.0)
     slab[...] = total
     for k in steps:
         gather_copy(k).start()
     ens[m] = total
+    pres = jnp.where(owned, cur_buf[...] + scale * far, pres)
+    end_mean(0)
+    first_means = [mean_of(0, i) for i in range(n_mem)]
+    first_mean = mean_of(0, m)
+    current = pres - over_cells(first_mean)
+    lowered = over_cells(sum(first_means))
     end_mean(1)
-    p_out[...] = less_mean(current, mean_of(1, m) - mean_of(0, m))
-    all_means = mean_of(1, 0) - mean_of(0, 0)
+    p_out[...] = current - over_cells(mean_of(1, m) - first_mean)
+    all_means = mean_of(1, 0) - first_means[0]
     for i in range(1, n_mem):
-        all_means = all_means + (mean_of(1, i) - mean_of(0, i))
+        all_means = all_means + (mean_of(1, i) - first_means[i])
+    all_means = over_cells(all_means)
     others = ens.at[pl.ds(0, n_mem - 1)]
     pltpu.make_async_copy(others, others, x_recv.at[1]).wait()
-    summed = jnp.concatenate([ens[i] for i in range(n_mem)], axis=0)
-    e_out[...] = less_mean(summed, all_means) / n_mem
+    summed = jnp.concatenate([ens[i] for i in range(n_mem)], axis=0) - lowered
+    e_out[...] = (summed - all_means) / n_mem
 
     pltpu.make_async_copy(snd, snd, s_send).wait()
-    pltpu.make_async_copy(reach, reach, h_sem.at[0]).wait()
+    pltpu.make_async_copy(reach, reach, h_send).wait()
+    sent = zbox.at[pl.ds(0, n_mem - 1)]
+    pltpu.make_async_copy(sent, sent, z_send).wait()
     sent = box_a.at[:, pl.ds(0, LINE - 1)]
     pltpu.make_async_copy(sent, sent, a_send).wait()
     sent = box_x.at[:, pl.ds(0, len(shifts))]
@@ -487,20 +537,25 @@
             pltpu.VMEM((3, 8, CC), F32),
             pltpu.VMEM((8, NBK, LV, HB), F32),
             pltpu.VMEM((8, NBK, LV, HB), F32),
-            pltpu.VMEM((NBK, 1, HB), F32),
-            pltpu.VMEM((NBK, 1, HB), F32),
+            pltpu.VMEM((2, NBK, 1, HB), F32),
+            pltpu.VMEM((2, NBK, 1, HB), F32),
             pltpu.VMEM((2, 1, HB), F32),
             pltpu.VMEM((2, 1, HB), F32),
             pltpu.VMEM((2, LINE, 1, HB), F32),
             pltpu.VMEM((2, n_all, 1, HB), F32),
+            pltpu.VMEM((NBK, LV, HB), F32),
+            pltpu.VMEM((n_mem, NBK, band, HB), F32),
             pltpu.VMEM((LV, CC), F32),
             pltpu.VMEM((n_mem, band, CC), F32),
             pltpu.VMEM((band, CC), F32),
             pltpu.VMEM((n_mem, band, CC), F32),
             dma((10,)),
             dma,
-            dma((8, 2)),
+            dma((8,)),
+            dma,
             dma((2,)),
+            dma,
+            dma,
             dma,
             dma((2,)),
             dma,

time: 52.7 us -> 53 us (level)
  Pallas kernels: 51.5 us -> 52.2 us
    pallas_call x1, Pallas kernels: 50.7 us -> 51.5 us  [per_device(): pl.pallas_call(kernel, out_shape=tuple((pltpu.VMEM((LV, CC), F32) for _ i...]
where the time goes in v4:
time: 53 us; the launch traced here: 52.9 us
  Pallas kernels  52.2 us (98%)
  between operations  0.64 us (1%)
    pallas_call x1, Pallas kernels, per_device(): pl.pallas_call(kernel, out_shape=tuple((pltpu.VMEM((LV, CC), F32) for _ i...  51.5 us

profile of v4, /device:TPU:1, one launch (start us, length us, event | category | flops | bytes accessed | tf_op | source)
XLA Modules:
  0.0 52.9 jit_solution(6214593789144538448)
XLA Ops:
  0.6 51.5 %shard_map.121 = (f32[32,1024]{1,0:T(8,128)S(1)}, f32[32,1024]{1,0:T(8,128)S(1)}, f32[32,1024]{1,0:T(8,128)S(1)}) custom-call(f32[1,4]{1,0:T(1,128)} %par_hbm.1, f32[1,32,1024]{2,1,0:T(8,128)} %p_hbm.1, f32[1,32,1024]{2,1,0:T(8,128)} %q_hbm.1, f32[1,32,1024]{2,1,0:T(8,128)} %t_hbm.1, f32[32,3072]{1,0:T(8,128)} %v_hbm.1, f32[1,3072]{1,0:T(1,128)} %bitcast.4, ...), custom_call_target="tpu_custom_call" | custom-call | tf_op jit(solution)/shard_map/pallas_call | solution.py:518
  52.1 0.8 %shard_map.122 = (f32[1,32,1024]{2,1,0:T(8,128)}, f32[1,32,1024]{2,1,0:T(8,128)}, f32[32,1024]{1,0:T(8,128)}) custom-call(f32[32,1024]{1,0:T(8,128)S(1)} %get-tuple-element.6.p, f32[32,1024]{1,0:T(8,128)S(1)} %get-tuple-element.7.t, f32[32,1024]{1,0:T(8,128)S(1)} %get-tuple-element.8.e), custom_call_target="tpu_custom_call" | custom-call | tf_op jit(solution)/shard_map/pallas_call | solution.py:579

commit v5 on v4

--- a/solution.py
+++ b/solution.py
@@ -58,7 +58,7 @@
     p_out, t_out, e_out,
     par, p_in, q_in, t_in, v_in, len_in, met_in, inv_in, exp_in, end_in,
     sel, esel, vd, sd, snd, rcv, reach, reach_in, row_a, row_b, box_a, box_x, zsnd, zbox, cur_buf, rs_box, slab, ens,
-    in_sem, s_send, s_recv, h_send, h_recv, z_send, z_recv, a_send, a_recv, b_send, b_recv, x_send, x_recv,
+    in_sem, s_send, s_recv, h_send, h_recv, z_send, z_recv, token, a_send, a_recv, b_send, b_recv, x_send, x_recv,
 ):
     n_mem = lax.axis_size("member")
     n_dom = lax.axis_size("dom")
@@ -82,8 +82,9 @@
     across = [((m + i) % n_mem, (d + k * LINE) % n_dom) for i, k in shifts]
 
     barrier = pltpu.get_barrier_semaphore()
-    peers = neighbours + in_line + across
-    peers += [((m + i) % n_mem, p) for i in range(1, n_mem) for _, p in neighbours]
+    members = [((m + i) % n_mem, d) for i in range(1, n_mem)]
+    peers = neighbours + [in_line[k - 1] for k in (1, 2, 3, LINE - 3, LINE - 2, LINE - 1)]
+    peers += members + [(m, (d + k * LINE) % n_dom) for k in range(1, n_line)]
     for peer in peers:
         pl.semaphore_signal(barrier, inc=1, device_id=peer, device_id_type=MESH)
 
@@ -127,19 +128,18 @@
             device_id_type=MESH,
         )
 
-    def export_and_send(*slots_and_fields):
+    def stage(*slots_and_fields):
         slots, fields = slots_and_fields[::2], slots_and_fields[1::2]
         o = mm(rows2(*fields), esel[...])
         for i, slot in enumerate(slots):
             values = fold(o, i)
             for b in range(NBK):
                 snd[slot, b] = values[:, b * HB : (b + 1) * HB]
-        if slots[0] == 6:
-            pl.semaphore_wait(barrier, len(peers))
-        for slot in slots:
-            for b in SEND_ORDER:
-                halo_copy(slot, b).start()
         return fold(o)
+
+    def start(slot):
+        for b in SEND_ORDER:
+            halo_copy(slot, b).start()
 
     def arrived(slot):
         pltpu.make_async_copy(rcv.at[slot], rcv.at[slot], s_recv.at[slot]).wait()
@@ -148,7 +148,12 @@
     loaded(1)
     theta = t_in[...]
     pres = p_in[...]
-    export_and_send(6, theta, 0, pres)
+    stage(6, theta, 0, pres)
+    pl.semaphore_wait(barrier, len(peers))
+    start(6)
+    start(0)
+    for member in members:
+        pl.semaphore_signal(token, inc=1, device_id=member, device_id_type=MESH)
 
     loaded(2)
     ends = end_in[1:2, :]
@@ -223,8 +228,10 @@
             nets = [net + flow - part(incoming, i) for i, (net, flow) in enumerate(zip(nets, flows))]
         return nets
 
-    def far_pressure(slot, net):
+    def far_pressure(slot, net, late=None):
         lhs = rows2(arrived(slot))
+        if late is not None:
+            start(late)
         for j in range(3):
             net = net + weight(j) * fold(mm(lhs, sel[j, CC:, :]))
         return net
@@ -260,10 +267,10 @@
             p[:, g * HB : (g + 1) * HB] * factor[:, g * HB : (g + 1) * HB] for g in range(CC // HB)
         )
 
-    def partial_row(total):
+    def partial_row(total, later):
         spread = by_lane(jnp.ones((1, CC), F32), area)
-        padded = jnp.concatenate([total, spread, jnp.zeros((HB - LV - 1, HB), F32)], axis=0)
-        return jnp.sum(padded.T, axis=0, keepdims=True)
+        parts = [total, spread, jnp.zeros((LV - 1, HB), F32), later, jnp.zeros((LV, HB), F32)]
+        return jnp.sum(jnp.concatenate(parts, axis=0).T, axis=0, keepdims=True)
 
     def reach_copy(which, b):
         return pltpu.make_async_remote_copy(
@@ -297,58 +304,52 @@
         block = sd[j, 0:1, :]
         return jnp.where((block >= CC // 256) & (block < EXT // 256), weight(j), 0.0)
 
-    def spread_row(row):
-        return jnp.broadcast_to(row, (HB, HB)).T[:LV]
-
-    def line_copy(which, k):
+    def line_copy(k):
         return pltpu.make_async_remote_copy(
-            src_ref=row_a.at[which],
-            dst_ref=box_a.at[which, pos],
+            src_ref=row_a,
+            dst_ref=box_a.at[pos],
             send_sem=a_send,
-            recv_sem=a_recv.at[which],
+            recv_sem=a_recv,
             device_id=in_line[k],
             device_id_type=MESH,
         )
 
-    def wide_copy(which, n):
+    def wide_copy(n):
         return pltpu.make_async_remote_copy(
-            src_ref=row_b.at[which],
-            dst_ref=box_x.at[which, m * n_line + line],
+            src_ref=row_b,
+            dst_ref=box_x.at[m * n_line + line],
             send_sem=b_send,
-            recv_sem=b_recv.at[which],
+            recv_sem=b_recv,
             device_id=across[n],
             device_id_type=MESH,
         )
 
-    def start_mean(which, total):
-        row = partial_row(total)
-        row_a[which] = row
+    def start_means(row):
+        row_a[...] = row
         for k in range(LINE - 1):
-            line_copy(which, k).start()
-        box_a[which, pos] = row
-
-    def turn_mean(which):
-        others = box_a.at[which, pl.ds(0, LINE - 1)]
-        pltpu.make_async_copy(others, others, a_recv.at[which]).wait()
-        row = jnp.sum(box_a[which], axis=0)
-        row_b[which] = row
+            line_copy(k).start()
+        box_a[pos] = row
+
+    def turn_means():
+        others = box_a.at[pl.ds(0, LINE - 1)]
+        pltpu.make_async_copy(others, others, a_recv).wait()
+        row = jnp.sum(box_a[...], axis=0)
+        row_b[...] = row
         for n in range(len(shifts)):
-            wide_copy(which, n).start()
-        box_x[which, m * n_line + line] = row
-
-    def end_mean(which):
-        others = box_x.at[which, pl.ds(0, len(shifts))]
-        pltpu.make_async_copy(others, others, b_recv.at[which]).wait()
-
-    def mean_of(which, member):
-        return level_mean(box_x[which, pl.ds(member * n_line, n_line)])
-
-    def level_mean(rows):
-        row = jnp.sum(rows, axis=0)
+            wide_copy(n).start()
+        box_x[m * n_line + line] = row
+
+    def means_of(member):
+        row = jnp.sum(box_x[pl.ds(member * n_line, n_line)], axis=0)
         return row / row[:, LV : LV + 1]
 
-    def over_cells(mean):
-        return jnp.where(owned, jnp.concatenate([spread_row(mean)] * (CC // HB), axis=1), 0.0)
+    def over_cells(column):
+        return jnp.where(owned, jnp.concatenate([column] * (CC // HB), axis=1), 0.0)
+
+    def both_means(row):
+        columns = jnp.broadcast_to(row, (HB, HB)).T
+        first = columns[:LV]
+        return over_cells(first), over_cells(columns[2 * LV : 3 * LV] - first)
 
     for t in range(CC // 256, EXT // 256):
         build_tile(t, float(t), t * 256)
@@ -358,19 +359,22 @@
     force = couple * (theta_next - theta) / NS
     theta = theta_next
     pres, prev = advance(pres, q_in[...], net, force)
-    export_and_send(1, pres)
-    export_and_send(7, theta)
+    stage(1, pres)
+    start(1)
+    stage(7, theta)
     send_reach(0, [weight(j) for j in range(3)])
     (net,) = near(pres)
-    pres, prev = advance(pres, prev, far_pressure(1, net), force)
-    export_and_send(2, pres)
+    pres, prev = advance(pres, prev, far_pressure(1, net, late=7), force)
+    stage(2, pres)
+    start(2)
     net, net_theta = near(pres, theta, theta_last=True)
     once = reached(0) - halo_weight(0) - halo_weight(1) - halo_weight(2)
     scaled = jnp.where(owned, once * inv, 0.0)
     send_reach(1, [weight(j) * scaled for j in range(3)])
     pres, prev = advance(pres, prev, far_pressure(2, net), force)
-    export_and_send(3, pres)
-    start_mean(0, by_lane(pres, area))
+    stage(3, pres)
+    start(3)
+    first_sums = by_lane(pres, area)
     net, twice = near(pres, jnp.concatenate([scaled, jnp.zeros((7, CC), F32)], axis=0))
     twice = twice[0:1] + reached(1)
     theta_next = advance_theta(theta, far_theta(7, net_theta))
@@ -380,10 +384,11 @@
     by_q = 2.0 * area + speed * once
     by_f = 3.0 * area + speed * once
     pres, prev = advance(pres, prev, far_pressure(3, net), force)
-    export_and_send(4, pres)
-    start_mean(1, by_lane(pres, by_p) - by_lane(prev, by_q) + by_lane(force, by_f))
+    stage(4, pres)
+    start(4)
+    later_sums = by_lane(pres, by_p) - by_lane(prev, by_q) + by_lane(force, by_f)
+    start_means(partial_row(first_sums, later_sums))
     (net,) = near(pres)
-    turn_mean(0)
     pres, prev = advance(pres, prev, far_pressure(4, net), force)
 
     band = LV // n_mem
@@ -424,9 +429,11 @@
             device_id_type=MESH,
         )
 
-    values = speed * export_and_send(5, pres)
+    values = speed * stage(5, pres)
+    start(5)
     for b in range(NBK):
         zsnd[b] = values[:, b * HB : (b + 1) * HB]
+    pl.semaphore_wait(token, n_mem - 1)
     for k in steps:
         for b in SEND_ORDER:
             sum_copy(k, b).start()
@@ -435,7 +442,7 @@
     for k in steps:
         scatter_copy(k).start()
     rs_box[m] = cur_buf[band_of(m), :]
-    turn_mean(1)
+    turn_means()
     far = far_pressure(5, jnp.zeros((LV, CC), F32))
     for b in range(NBK):
         zbox[m, b] = speed * rcv[5, b, band_of(m), :]
@@ -454,29 +461,23 @@
         gather_copy(k).start()
     ens[m] = total
     pres = jnp.where(owned, cur_buf[...] + scale * far, pres)
-    end_mean(0)
-    first_means = [mean_of(0, i) for i in range(n_mem)]
-    first_mean = mean_of(0, m)
-    current = pres - over_cells(first_mean)
-    lowered = over_cells(sum(first_means))
-    end_mean(1)
-    p_out[...] = current - over_cells(mean_of(1, m) - first_mean)
-    all_means = mean_of(1, 0) - first_means[0]
-    for i in range(1, n_mem):
-        all_means = all_means + (mean_of(1, i) - first_means[i])
-    all_means = over_cells(all_means)
+    others = box_x.at[pl.ds(0, len(shifts))]
+    pltpu.make_async_copy(others, others, b_recv).wait()
+    first, second = both_means(means_of(m))
+    p_out[...] = (pres - first) - second
+    first, second = both_means(sum(means_of(i) for i in range(n_mem)))
     others = ens.at[pl.ds(0, n_mem - 1)]
     pltpu.make_async_copy(others, others, x_recv.at[1]).wait()
-    summed = jnp.concatenate([ens[i] for i in range(n_mem)], axis=0) - lowered
-    e_out[...] = (summed - all_means) / n_mem
+    summed = jnp.concatenate([ens[i] for i in range(n_mem)], axis=0)
+    e_out[...] = ((summed - first) - second) / n_mem
 
     pltpu.make_async_copy(snd, snd, s_send).wait()
     pltpu.make_async_copy(reach, reach, h_send).wait()
     sent = zbox.at[pl.ds(0, n_mem - 1)]
     pltpu.make_async_copy(sent, sent, z_send).wait()
-    sent = box_a.at[:, pl.ds(0, LINE - 1)]
+    sent = box_a.at[pl.ds(0, LINE - 1)]
     pltpu.make_async_copy(sent, sent, a_send).wait()
-    sent = box_x.at[:, pl.ds(0, len(shifts))]
+    sent = box_x.at[pl.ds(0, len(shifts))]
     pltpu.make_async_copy(sent, sent, b_send).wait()
     sent = ens.at[pl.ds(0, n_mem - 1)]
     for phase in range(2):
@@ -539,10 +540,10 @@
             pltpu.VMEM((8, NBK, LV, HB), F32),
             pltpu.VMEM((2, NBK, 1, HB), F32),
             pltpu.VMEM((2, NBK, 1, HB), F32),
-            pltpu.VMEM((2, 1, HB), F32),
-            pltpu.VMEM((2, 1, HB), F32),
-            pltpu.VMEM((2, LINE, 1, HB), F32),
-            pltpu.VMEM((2, n_all, 1, HB), F32),
+            pltpu.VMEM((1, HB), F32),
+            pltpu.VMEM((1, HB), F32),
+            pltpu.VMEM((LINE, 1, HB), F32),
+            pltpu.VMEM((n_all, 1, HB), F32),
             pltpu.VMEM((NBK, LV, HB), F32),
             pltpu.VMEM((n_mem, NBK, band, HB), F32),
             pltpu.VMEM((LV, CC), F32),
@@ -556,10 +557,11 @@
             dma((2,)),
             dma,
             dma,
-            dma,
-            dma((2,)),
-            dma,
-            dma((2,)),
+            pltpu.SemaphoreType.REGULAR,
+            dma,
+            dma,
+            dma,
+            dma,
             dma((2,)),
             dma((2,)),
         ],

time: 53 us -> 50.6 us (0.955)
  Pallas kernels: 52.2 us -> 49.9 us
    pallas_call x1, Pallas kernels: 51.5 us -> 49.1 us  [per_device(): pl.pallas_call(kernel, out_shape=tuple((pltpu.VMEM((LV, CC), F32) for _ i...]
where the time goes in v5:
time: 50.6 us; the launch traced here: 50.5 us
  Pallas kernels  49.9 us (99%)
  between operations  0.64 us (1%)
    pallas_call x1, Pallas kernels, per_device(): pl.pallas_call(kernel, out_shape=tuple((pltpu.VMEM((LV, CC), F32) for _ i...  49.1 us

profile of v5, /device:TPU:1, one launch (start us, length us, event | category | flops | bytes accessed | tf_op | source)
XLA Modules:
  0.0 50.5 jit_solution(10729982796220136855)
XLA Ops:
  0.6 49.1 %shard_map.121 = (f32[32,1024]{1,0:T(8,128)S(1)}, f32[32,1024]{1,0:T(8,128)S(1)}, f32[32,1024]{1,0:T(8,128)S(1)}) custom-call(f32[1,4]{1,0:T(1,128)} %par_hbm.1, f32[1,32,1024]{2,1,0:T(8,128)} %p_hbm.1, f32[1,32,1024]{2,1,0:T(8,128)} %q_hbm.1, f32[1,32,1024]{2,1,0:T(8,128)} %t_hbm.1, f32[32,3072]{1,0:T(8,128)} %v_hbm.1, f32[1,3072]{1,0:T(1,128)} %bitcast.4, ...), custom_call_target="tpu_custom_call" | custom-call | tf_op jit(solution)/shard_map/pallas_call | solution.py:519
  49.8 0.8 %shard_map.122 = (f32[1,32,1024]{2,1,0:T(8,128)}, f32[1,32,1024]{2,1,0:T(8,128)}, f32[32,1024]{1,0:T(8,128)}) custom-call(f32[32,1024]{1,0:T(8,128)S(1)} %get-tuple-element.6.p, f32[32,1024]{1,0:T(8,128)S(1)} %get-tuple-element.7.t, f32[32,1024]{1,0:T(8,128)S(1)} %get-tuple-element.8.e), custom_call_target="tpu_custom_call" | custom-call | tf_op jit(solution)/shard_map/pallas_call | solution.py:581

commit v6 on v5

--- a/solution.py
+++ b/solution.py
@@ -67,6 +67,15 @@
     d = lax.axis_index("dom")
     line, pos = d // LINE, d % LINE
 
+    neighbours = [(m, (d + off + n_dom) % n_dom) for off in OFFSETS]
+    in_line = [(m, line * LINE + (pos + k) % LINE) for k in range(1, LINE)]
+    shifts = [(i, k) for i in range(n_mem) for k in range(n_line) if i or k]
+    across = [((m + i) % n_mem, (d + k * LINE) % n_dom) for i, k in shifts]
+
+    barrier = pltpu.get_barrier_semaphore()
+    for peer in neighbours:
+        pl.semaphore_signal(barrier, inc=1, device_id=peer, device_id_type=MESH)
+
     sources = (exp_hbm, t_hbm.at[0], p_hbm.at[0], end_hbm, len_hbm, met_hbm, v_hbm, inv_hbm, par_hbm, q_hbm.at[0])
     targets = (exp_in, t_in, p_in, end_in, len_in, met_in, v_in, inv_in, par, q_in)
     groups = (0, 1, 1, 2, 2, 2, 3, 3, 3, 3)
@@ -76,16 +85,10 @@
     for load in loads:
         load.start()
 
-    neighbours = [(m, (d + off + n_dom) % n_dom) for off in OFFSETS]
-    in_line = [(m, line * LINE + (pos + k) % LINE) for k in range(1, LINE)]
-    shifts = [(i, k) for i in range(n_mem) for k in range(n_line) if i or k]
-    across = [((m + i) % n_mem, (d + k * LINE) % n_dom) for i, k in shifts]
-
-    barrier = pltpu.get_barrier_semaphore()
     members = [((m + i) % n_mem, d) for i in range(1, n_mem)]
     peers = neighbours + [in_line[k - 1] for k in (1, 2, 3, LINE - 3, LINE - 2, LINE - 1)]
     peers += members + [(m, (d + k * LINE) % n_dom) for k in range(1, n_line)]
-    for peer in peers:
+    for peer in peers[len(neighbours) :]:
         pl.semaphore_signal(barrier, inc=1, device_id=peer, device_id_type=MESH)
 
     def loaded(group):
@@ -430,13 +433,13 @@
         )
 
     values = speed * stage(5, pres)
-    start(5)
     for b in range(NBK):
         zsnd[b] = values[:, b * HB : (b + 1) * HB]
     pl.semaphore_wait(token, n_mem - 1)
     for k in steps:
         for b in SEND_ORDER:
             sum_copy(k, b).start()
+    start(5)
     (net,) = near(pres)
     cur_buf[...] = advance(pres, prev, net, force)[0]
     for k in steps:

time: 50.6 us -> 50.4 us (level)
  no operation moved by 1% of the time
where the time goes in v6:
time: 50.4 us; the launch traced here: 50.3 us
  Pallas kernels  49.7 us (99%)
  between operations  0.64 us (1%)
    pallas_call x1, Pallas kernels, per_device(): pl.pallas_call(kernel, out_shape=tuple((pltpu.VMEM((LV, CC), F32) for _ i...  48.9 us

profile of v6, /device:TPU:1, one launch (start us, length us, event | category | flops | bytes accessed | tf_op | source)
XLA Modules:
  0.0 50.3 jit_solution(9346169057057895670)
XLA Ops:
  0.6 48.9 %shard_map.121 = (f32[32,1024]{1,0:T(8,128)S(1)}, f32[32,1024]{1,0:T(8,128)S(1)}, f32[32,1024]{1,0:T(8,128)S(1)}) custom-call(f32[1,4]{1,0:T(1,128)} %par_hbm.1, f32[1,32,1024]{2,1,0:T(8,128)} %p_hbm.1, f32[1,32,1024]{2,1,0:T(8,128)} %q_hbm.1, f32[1,32,1024]{2,1,0:T(8,128)} %t_hbm.1, f32[32,3072]{1,0:T(8,128)} %v_hbm.1, f32[1,3072]{1,0:T(1,128)} %bitcast.4, ...), custom_call_target="tpu_custom_call" | custom-call | tf_op jit(solution)/shard_map/pallas_call | solution.py:522
  49.5 0.8 %shard_map.122 = (f32[1,32,1024]{2,1,0:T(8,128)}, f32[1,32,1024]{2,1,0:T(8,128)}, f32[32,1024]{1,0:T(8,128)}) custom-call(f32[32,1024]{1,0:T(8,128)S(1)} %get-tuple-element.6.p, f32[32,1024]{1,0:T(8,128)S(1)} %get-tuple-element.7.t, f32[32,1024]{1,0:T(8,128)S(1)} %get-tuple-element.8.e), custom_call_target="tpu_custom_call" | custom-call | tf_op jit(solution)/shard_map/pallas_call | solution.py:584

commit v7 on v6

--- a/solution.py
+++ b/solution.py
@@ -20,7 +20,7 @@
 DT = 0.25
 NS = 3
 OFFSETS = [(b // 2 + 1) * (1 - 2 * (b % 2)) for b in range(NBK)]
-SEND_ORDER = (4, 5, 2, 3, 0, 1)
+SEND_ORDER = (4, 5, 0, 1, 2, 3)
 
 
 def split2(x):
@@ -245,14 +245,6 @@
             net = net + coefficients(j)[1] * fold(mm(lhs, sel[j, CC:, :]))
         return net
 
-    def far_both(slot_p, net_p, slot_t, net_t):
-        lhs = rows2(arrived(slot_p), arrived(slot_t))
-        for j in range(3):
-            o = mm(lhs, sel[j, CC:, :])
-            net_p = net_p + weight(j) * fold(o, 0)
-            net_t = net_t + coefficients(j)[1] * fold(o, 1)
-        return net_p, net_t
-
     def advance_theta(th, net):
         up = jnp.concatenate([th[1:], th[LV - 1 :]], axis=0) - th
         down = th - jnp.concatenate([th[:1], th[: LV - 1]], axis=0)
@@ -357,11 +349,10 @@
     for t in range(CC // 256, EXT // 256):
         build_tile(t, float(t), t * 256)
     net, net_theta = near(pres, theta, theta_last=True)
-    net, net_theta = far_both(0, net, 6, net_theta)
-    theta_next = advance_theta(theta, net_theta)
+    theta_next = advance_theta(theta, far_theta(6, net_theta))
     force = couple * (theta_next - theta) / NS
     theta = theta_next
-    pres, prev = advance(pres, q_in[...], net, force)
+    pres, prev = advance(pres, q_in[...], far_pressure(0, net), force)
     stage(1, pres)
     start(1)
     stage(7, theta)

time: 50.4 us -> 49.7 us (0.986)
  Pallas kernels: 49.7 us -> 49 us
    pallas_call x1, Pallas kernels: 48.9 us -> 48.2 us  [per_device(): pl.pallas_call(kernel, out_shape=tuple((pltpu.VMEM((LV, CC), F32) for _ i...]
where the time goes in v7:
time: 49.7 us; the launch traced here: 49.6 us
  Pallas kernels  49 us (99%)
  between operations  0.64 us (1%)
    pallas_call x1, Pallas kernels, per_device(): pl.pallas_call(kernel, out_shape=tuple((pltpu.VMEM((LV, CC), F32) for _ i...  48.2 us

profile of v7, /device:TPU:1, one launch (start us, length us, event | category | flops | bytes accessed | tf_op | source)
XLA Modules:
  0.0 49.6 jit_solution(14592318482985479319)
XLA Ops:
  0.6 48.2 %shard_map.121 = (f32[32,1024]{1,0:T(8,128)S(1)}, f32[32,1024]{1,0:T(8,128)S(1)}, f32[32,1024]{1,0:T(8,128)S(1)}) custom-call(f32[1,4]{1,0:T(1,128)} %par_hbm.1, f32[1,32,1024]{2,1,0:T(8,128)} %p_hbm.1, f32[1,32,1024]{2,1,0:T(8,128)} %q_hbm.1, f32[1,32,1024]{2,1,0:T(8,128)} %t_hbm.1, f32[32,3072]{1,0:T(8,128)} %v_hbm.1, f32[1,3072]{1,0:T(1,128)} %bitcast.4, ...), custom_call_target="tpu_custom_call" | custom-call | tf_op jit(solution)/shard_map/pallas_call | solution.py:513
  48.8 0.8 %shard_map.122 = (f32[1,32,1024]{2,1,0:T(8,128)}, f32[1,32,1024]{2,1,0:T(8,128)}, f32[32,1024]{1,0:T(8,128)}) custom-call(f32[32,1024]{1,0:T(8,128)S(1)} %get-tuple-element.6.p, f32[32,1024]{1,0:T(8,128)S(1)} %get-tuple-element.7.t, f32[32,1024]{1,0:T(8,128)S(1)} %get-tuple-element.8.e), custom_call_target="tpu_custom_call" | custom-call | tf_op jit(solution)/shard_map/pallas_call | solution.py:575
